TPU v7x, 16 devices: a 4x2x1 block of a 4x4x8 slice. The times are simulated.
16 devices in a mesh: rep: 2 (over y, z), dp: 8 (over x, core).
Axes of the slice: x: 4, y: 2, z: 1, core: 2. Of those that a mesh axis runs over, the one named last changes fastest.
The devices are a block of a 4x4x8 slice.
Arguments:
- x: bfloat16 [16, 2048, 1024], P(('rep', 'dp')), parts along dimension 0
- dy: bfloat16 [16, 2048, 1024], P(('rep', 'dp')), parts along dimension 0
- w_gate: bfloat16 [2, 1024, 2560], P(None, 'dp')
- w_up: bfloat16 [2, 1024, 2560], P(None, 'dp')
- w_down: bfloat16 [2, 2560, 1024], P(None, 'dp')
- m_w_gate: float32 [2, 1024, 2560], P(None, 'dp')
- m_w_up: float32 [2, 1024, 2560], P(None, 'dp')
- m_w_down: float32 [2, 2560, 1024], P(None, 'dp')
- v_w_gate: float32 [2, 1024, 2560], P(None, 'dp')
- v_w_up: float32 [2, 1024, 2560], P(None, 'dp')
- v_w_down: float32 [2, 2560, 1024], P(None, 'dp')
Outputs:
- output 1: bfloat16 [4, 1024, 2560], P('rep', 'dp'), parts along dimension 0
- output 2: bfloat16 [4, 1024, 2560], P('rep', 'dp'), parts along dimension 0
- output 3: bfloat16 [4, 2560, 1024], P('rep', 'dp'), parts along dimension 0
- output 4: float32 [4, 1024, 2560], P('rep', 'dp'), parts along dimension 0
- output 5: float32 [4, 1024, 2560], P('rep', 'dp'), parts along dimension 0
- output 6: float32 [4, 2560, 1024], P('rep', 'dp'), parts along dimension 0
- output 7: float32 [4, 1024, 2560], P('rep', 'dp'), parts along dimension 0
- output 8: float32 [4, 1024, 2560], P('rep', 'dp'), parts along dimension 0
- output 9: float32 [4, 2560, 1024], P('rep', 'dp'), parts along dimension 0
There are 2 independent parts. A program takes and returns all parts, laid end to end along the dimension named above; an argument that names none is the same for every part.
All inputs are finite; a program needn't handle non-finite values.
Results may differ from a plain program's by a relative error of at most 0.022.
Values are sent between devices in bfloat16 or wider.
A program may use at most 768 MiB of HBM per device.

v0:
```python
import jax
import jax.numpy as jnp
from jax import lax
from jax.sharding import PartitionSpec as P

NAMES = ("w_gate", "w_up", "w_down")


def matmul(a, w):
    return jnp.dot(a, w, preferred_element_type=jnp.float32).astype(jnp.bfloat16)


def normed(h):
    wide = h.astype(jnp.float32)
    scale = lax.rsqrt(jnp.mean(wide**2, -1, keepdims=True) + 1e-6)
    return (wide * scale).astype(jnp.bfloat16)


def layer(h, w):
    a = normed(h)
    gate = jnp.dot(a, w["w_gate"], preferred_element_type=jnp.float32)
    up = jnp.dot(a, w["w_up"], preferred_element_type=jnp.float32)
    return h + matmul((jax.nn.silu(gate) * up).astype(jnp.bfloat16), w["w_down"])


def adamw(w, m, v, g):
    m = 0.9 * m + 0.1 * g
    v = 0.95 * v + 0.05 * g * g
    step = m * lax.rsqrt(v + 1e-8) + 0.1 * w
    return (w - 0.02 * step).astype(jnp.bfloat16), m, v


def clipped(gradients, sum_of_squares, count):
    factor = jnp.minimum(1.0, 0.5 * lax.rsqrt(sum_of_squares / count + 1e-30))
    return [g * factor for g in gradients]


def solution(mesh):
    def fetched(weights, number):
        return {name: lax.all_gather(w[number], "dp", axis=0, tiled=True) for name, w in zip(NAMES, weights, strict=True)}

    def step(x, dy, *arrays):
        weights, m, v = (arrays[i : i + 3] for i in (0, 3, 6))
        layers = weights[0].shape[0]
        h, kept = x[0], []
        for number in range(layers):
            kept.append(h)
            h = layer(h, fetched(weights, number))
        by_h, mine = dy[0], [None] * layers
        for number in reversed(range(layers)):
            _, back = jax.vjp(lambda w, h: layer(h, w), fetched(weights, number), kept[number])
            by_w, by_h = back(by_h)
            mine[number] = [lax.psum_scatter(by_w[name], "dp", scatter_dimension=0, tiled=True) for name in NAMES]
        gradients = [jnp.stack([mine[number][i] for number in range(layers)]).astype(jnp.float32) for i in range(3)]
        squares = lax.psum(sum(jnp.sum(g * g) for g in gradients), "dp")
        gradients = clipped(gradients, squares, lax.psum(1, "dp") * sum(g.size for g in gradients))
        new = [adamw(w.astype(jnp.float32), m, v, g) for w, m, v, g in zip(weights, m, v, gradients, strict=True)]
        return tuple(one[which] for which in range(3) for one in new)

    states, cut = P(("rep", "dp"), None, None), P(None, "dp", None)
    return jax.shard_map(
        step,
        mesh=mesh,
        in_specs=(states, states) + (cut,) * 9,
        out_specs=(P("rep", "dp", None),) * 9,
        check_vma=False,
    )
```

profile of v0, /device:TPU:113, one launch (start us, length us, event | category | flops | bytes accessed | tf_op | source)
XLA Modules:
  0.0 573.2 jit_solution(15868042940457215838)
XLA Ops:
  31.8 13.8 %all-gather.13.cloned.1.call-done = bf16[1,1024,2560]{2,1,0:T(8,128)(2,1)} async-done(((bf16[1,128,2560]{2,1,0:T(8,128)(2,1)}), bf16[1,1024,2560]{2,1,0:T(8,128)(2,1)}) %all-gather.13.cloned.1.call-update) | async-done | bytes 5242896 | tf_op jit(solution)/shard_map/all_gather | solution.py:40
  45.6 18.4 %fusion.41 = f32[2048,2560]{1,0:T(8,128)} fusion(bf16[1,1024,2560]{2,1,0:T(8,128)(2,1)} %all-gather.13.cloned.1.call-done, bf16[1,2048,1024]{1,2,0:T(8,128)(2,1)} %copy.20, f32[2048]{0:T(1024)S(1)} %add_rsqrt_fusion), kind=kOutput, calls=%fused_computation.59 | convolution fusion | flops 10743709696 | bytes 30416896 | tf_op jit(solution)/shard_map/dot_general | solution.py:21
  64.0 16.0 %all-gather.15.cloned.1.call-done = bf16[1,1024,2560]{2,1,0:T(8,128)(2,1)} async-done(((bf16[1,128,2560]{2,1,0:T(8,128)(2,1)}), bf16[1,1024,2560]{2,1,0:T(8,128)(2,1)}) %all-gather.15.cloned.1.call-update) | async-done | bytes 5242896 | tf_op jit(solution)/shard_map/all_gather | solution.py:40
  79.9 28.6 %multiply_convert_fusion.1 = (bf16[2048,2560]{1,0:T(8,128)(2,1)}, f32[2048,2560]{1,0:T(8,128)}) fusion(f32[2048,2560]{1,0:T(8,128)} %fusion.41, bf16[1,1024,2560]{2,1,0:T(8,128)(2,1)} %all-gather.15.cloned.1.call-done, bf16[1,2048,1024]{1,2,0:T(8,128)(2,1)} %copy.20, f32[2048]{0:T(1024)S(1)} %add_rsqrt_fusion), kind=kOutput, calls=%fused_computation.17 | convolution fusion | flops 10775166976 | bytes 61874176 | tf_op jit(solution)/shard_map/dot_general | solution.py:22
  114.3 17.9 %fusion.19 = (f32[2048]{0:T(1024)S(1)}, bf16[2048,1024]{0,1:T(8,128)(2,1)}) fusion(bf16[2048,2560]{1,0:T(8,128)(2,1)} %get-tuple-element.24, bf16[1,2560,1024]{2,1,0:T(8,128)(2,1)} %all-gather.17.cloned.1.call-done, bf16[1,2048,1024]{1,2,0:T(8,128)(2,1)} %copy.20), kind=kOutput, calls=%fused_computation.37 | convolution fusion | flops 10747901952 | bytes 24125440 | tf_op jit(solution)/shard_map/dot_general | solution.py:10
  132.7 15.7 %all-gather.21.cloned.1.call-done = bf16[1,2560,1024]{2,1,0:T(8,128)(2,1)} async-done(((bf16[1,320,1024]{2,1,0:T(8,128)(2,1)}), bf16[1,2560,1024]{2,1,0:T(8,128)(2,1)}) %all-gather.21.cloned.1.call-update) | async-done | bytes 5242896 | tf_op jit(solution)/shard_map/all_gather | solution.py:40
  148.5 17.1 %convolution_convert_fusion.1 = bf16[2048,2560]{1,0:T(8,128)(2,1)} fusion(bf16[1,2560,1024]{2,1,0:T(8,128)(2,1)} %all-gather.21.cloned.1.call-done, bf16[1,2048,1024]{2,1,0:T(8,128)(2,1)} %param.12), kind=kOutput, calls=%fused_computation.27 | convolution fusion | flops 10742661120 | bytes 19922944 | tf_op jit(solution)/shard_map/transpose(jvp())/dot_general | solution.py:10
  165.6 17.1 %all-gather.23.cloned.1.call-done = bf16[1,1024,2560]{2,1,0:T(8,128)(2,1)} async-done(((bf16[1,128,2560]{2,1,0:T(8,128)(2,1)}), bf16[1,1024,2560]{2,1,0:T(8,128)(2,1)}) %all-gather.23.cloned.1.call-update) | async-done | bytes 5242896 | tf_op jit(solution)/shard_map/all_gather | solution.py:40
  182.7 18.3 %fusion.28 = f32[2048,2560]{1,0:T(8,128)} fusion(bf16[1,1024,2560]{2,1,0:T(8,128)(2,1)} %all-gather.23.cloned.1.call-done, bf16[2048,1024]{0,1:T(8,128)(2,1)} %get-tuple-element.27, f32[2048]{0:T(1024)S(1)} %fusion.80), kind=kOutput, calls=%fused_computation.46 | convolution fusion | flops 10743709696 | bytes 30416896 | tf_op jit(solution)/shard_map/jvp()/dot_general | solution.py:22
  201.0 15.9 %all-gather.19.cloned.1.call-done = bf16[1,1024,2560]{2,1,0:T(8,128)(2,1)} async-done(((bf16[1,128,2560]{2,1,0:T(8,128)(2,1)}), bf16[1,1024,2560]{2,1,0:T(8,128)(2,1)}) %all-gather.19.cloned.1.call-update) | async-done | bytes 5242896 | tf_op jit(solution)/shard_map/all_gather | solution.py:40
  216.9 32.1 %fusion.2 = (bf16[2048,2560]{1,0:T(8,128)(2,1)}, f32[2048,2560]{1,0:T(8,128)}) fusion(f32[2048,2560]{1,0:T(8,128)} %fusion.28, bf16[2048,2560]{1,0:T(8,128)(2,1)} %convolution_convert_fusion.1, bf16[1,1024,2560]{2,1,0:T(8,128)(2,1)} %all-gather.19.cloned.1.call-done, bf16[2048,1024]{0,1:T(8,128)(2,1)} %get-tuple-element.27, f32[2048]{0:T(1024)S(1)} %fusion.80), kind=kOutput, calls=%fused_computation.8 | convolution fusion | flops 10806624256 | bytes 72359936 | tf_op jit(solution)/shard_map/jvp()/dot_general | solution.py:21
  249.0 20.0 %fusion.12 = bf16[2048,1024]{0,1:T(8,128)(2,1)} fusion(bf16[2048,2560]{1,0:T(8,128)(2,1)} %convolution_convert_fusion.1, bf16[1,1024,2560]{2,1,0:T(8,128)(2,1)} %all-gather.23.cloned.1.call-done, f32[2048,2560]{1,0:T(8,128)} %get-tuple-element.29), kind=kOutput, calls=%fused_computation.25 | convolution fusion | flops 10768875520 | bytes 40894464 | tf_op jit(solution)/shard_map/transpose(jvp())/dot_general | solution.py:22
  269.0 17.5 %fusion.21 = (f32[2048]{0:T(1024)S(1)}, bf16[2048,1024]{0,1:T(8,128)(2,1)S(1)}) fusion(bf16[2048,1024]{0,1:T(8,128)(2,1)} %get-tuple-element.27, bf16[2048,1024]{0,1:T(8,128)(2,1)} %fusion.12, bf16[2048,2560]{1,0:T(8,128)(2,1)} %get-tuple-element.28, bf16[1,1024,2560]{2,1,0:T(8,128)(2,1)} %all-gather.19.cloned.1.call-done), kind=kOutput, calls=%fused_computation.39 | convolution fusion | flops 10747901952 | bytes 28319744 | tf_op jit(solution)/shard_map/transpose(jvp())/dot_general | solution.py:21
  292.1 15.9 %convolution_convert_fusion.2 = bf16[2560,1024]{1,0:T(8,128)(2,1)} fusion(bf16[2048,2560]{1,0:T(8,128)(2,1)} %get-tuple-element.24, bf16[2048,1024]{0,1:T(8,128)(2,1)S(1)} %fusion.43), kind=kOutput, calls=%fused_computation.44 | convolution fusion | flops 10740039680 | bytes 19922944 | tf_op jit(solution)/shard_map/transpose(jvp())/dot_general | solution.py:10
  308.1 22.0 %fusion.22 = bf16[2560,1024]{1,0:T(8,128)(2,1)} fusion(f32[2048,2560]{1,0:T(8,128)} %fusion.28, bf16[1,2048,1024]{2,1,0:T(8,128)(2,1)} %param.12, f32[2048,2560]{1,0:T(8,128)} %get-tuple-element.29), kind=kOutput, calls=%fused_computation.40 | convolution fusion | flops 10771496960 | bytes 51380224 | tf_op jit(solution)/shard_map/transpose(jvp())/dot_general | solution.py:10
  330.2 17.2 %convolution_convert_fusion = bf16[2048,2560]{1,0:T(8,128)(2,1)} fusion(bf16[2048,1024]{0,1:T(8,128)(2,1)} %copy-done.6, bf16[1,2560,1024]{2,1,0:T(8,128)(2,1)} %all-gather.17.cloned.1.call-done), kind=kOutput, calls=%fused_computation.26 | convolution fusion | flops 10742661120 | bytes 19922944 | tf_op jit(solution)/shard_map/transpose(jvp())/dot_general | solution.py:10
  347.4 20.0 %fusion.27 = bf16[1024,2560]{1,0:T(8,128)(2,1)} fusion(bf16[2048,2560]{1,0:T(8,128)(2,1)} %convolution_convert_fusion, f32[2048,2560]{1,0:T(8,128)} %fusion.41, bf16[1,2048,1024]{1,2,0:T(8,128)(2,1)} %copy.20, f32[2048]{0:T(1024)S(1)} %copy-done.20), kind=kOutput, calls=%fused_computation.43 | convolution fusion | flops 10777788416 | bytes 40902656 | tf_op jit(solution)/shard_map/transpose(jvp())/dot_general | solution.py:22
  368.2 20.2 %fusion.23 = bf16[1024,2560]{1,0:T(8,128)(2,1)} fusion(bf16[2048,2560]{1,0:T(8,128)(2,1)} %convolution_convert_fusion.1, bf16[2048,1024]{0,1:T(8,128)(2,1)} %get-tuple-element.27, f32[2048]{0:T(1024)S(1)} %copy-done.16, f32[2048,2560]{1,0:T(8,128)} %get-tuple-element.29), kind=kOutput, calls=%fused_computation.41 | convolution fusion | flops 10777788416 | bytes 40902656 | tf_op jit(solution)/shard_map/transpose(jvp())/dot_general | solution.py:22
  388.5 24.8 %fusion.24 = bf16[1024,2560]{1,0:T(8,128)(2,1)} fusion(f32[2048,2560]{1,0:T(8,128)} %fusion.41, f32[2048,2560]{1,0:T(8,128)} %get-tuple-element.25, bf16[2048,2560]{1,0:T(8,128)(2,1)} %convolution_convert_fusion, bf16[1,2048,1024]{1,2,0:T(8,128)(2,1)} %copy.20, f32[2048]{0:T(1024)S(1)} %copy-done.20), kind=kOutput, calls=%fused_computation.42 | convolution fusion | flops 10804002816 | bytes 61874176 | tf_op jit(solution)/shard_map/transpose(jvp())/dot_general | solution.py:21
  413.4 16.8 %convolution_convert_fusion.3 = bf16[1024,2560]{1,0:T(8,128)(2,1)} fusion(bf16[2048,2560]{1,0:T(8,128)(2,1)} %get-tuple-element.28, bf16[2048,1024]{0,1:T(8,128)(2,1)} %get-tuple-element.27, f32[2048]{0:T(1024)S(1)} %copy-done.16), kind=kOutput, calls=%fused_computation.45 | convolution fusion | flops 10743709696 | bytes 19931136 | tf_op jit(solution)/shard_map/transpose(jvp())/dot_general | solution.py:21
  433.0 21.3 %reduce-scatter.13.cloned.1.call-done = bf16[128,2560]{1,0:T(8,128)(2,1)} async-done(((bf16[1024,2560]{1,0:T(8,128)(2,1)}), bf16[128,2560]{1,0:T(8,128)(2,1)}) %reduce-scatter.13.cloned.1.call-update) | async-done | bytes 655376 | tf_op jit(solution)/shard_map/reduce_scatter | solution.py:53
  456.8 35.1 %reduce-scatter.7.cloned.1.call-done = bf16[128,2560]{1,0:T(8,128)(2,1)} async-done(((bf16[1024,2560]{1,0:T(8,128)(2,1)}), bf16[128,2560]{1,0:T(8,128)(2,1)}) %reduce-scatter.7.cloned.1.call-update) | async-done | bytes 655376 | tf_op jit(solution)/shard_map/reduce_scatter | solution.py:53
  491.9 37.5 %reduce-scatter.9.cloned.1.call-done = bf16[128,2560]{1,0:T(8,128)(2,1)} async-done(((bf16[1024,2560]{1,0:T(8,128)(2,1)}), bf16[128,2560]{1,0:T(8,128)(2,1)}) %reduce-scatter.9.cloned.1.call-update) | async-done | bytes 655376 | tf_op jit(solution)/shard_map/reduce_scatter | solution.py:53
  534.1 15.6 %psum.7 = f32[]{:T(128)} all-reduce(f32[]{:T(128)S(6)} %add.99), channel_id=1, replica_groups=mesh['rep'=2,'dp'=8] {'dp'}, use_global_device_ids=true, to_apply=%region_12.13 | all-reduce | flops 1 | bytes 8 | tf_op jit(solution)/shard_map/psum | solution.py:55
  (85 shorter events, 61.0 us)
Async XLA Ops:
  7.2 38.4 %all-gather.13.cloned.1.call-start = ((), (), s32[]{:S(2)}) async-start(), calls=%async_computation.12 | async-start | bytes 5898240 | tf_op jit(solution)/shard_map/all_gather | solution.py:40
  9.8 70.1 %all-gather.15.cloned.1.call-start = ((), (), s32[]{:S(2)}) async-start(), calls=%async_computation.13 | async-start | bytes 5898240 | tf_op jit(solution)/shard_map/all_gather | solution.py:40
  12.4 101.9 %all-gather.17.cloned.1.call-start = ((), (), s32[]{:S(2)}) async-start(), calls=%async_computation.14 | async-start | bytes 5898240 | tf_op jit(solution)/shard_map/all_gather | solution.py:40
  13.7 134.8 %all-gather.21.cloned.1.call-start = ((), (), s32[]{:S(2)}) async-start(), calls=%async_computation.16 | async-start | bytes 5898240 | tf_op jit(solution)/shard_map/all_gather | solution.py:40
  14.3 168.3 %all-gather.23.cloned.1.call-start = ((), (), s32[]{:S(2)}) async-start(), calls=%async_computation.17 | async-start | bytes 5898240 | tf_op jit(solution)/shard_map/all_gather | solution.py:40
  15.0 201.9 %all-gather.19.cloned.1.call-start = ((), (), s32[]{:S(2)}) async-start(), calls=%async_computation.15 | async-start | bytes 5898240 | tf_op jit(solution)/shard_map/all_gather | solution.py:40
  15.6 414.7 %reduce-scatter.15.cloned.1.call-start = ((), (), s32[]{:S(2)}) async-start(), calls=%async_computation.10 | async-start | bytes 5898240 | tf_op jit(solution)/shard_map/reduce_scatter | solution.py:53
  25.3 54.7 %copy-start.19 = (f32[2048]{0:T(1024)}, f32[2048]{0:T(1024)S(1)}, u32[]{:S(2)}) copy-start(f32[2048]{0:T(1024)S(1)} %add_rsqrt_fusion) | copy-start | bytes 24580
  132.7 153.8 %copy-start.15 = (f32[2048]{0:T(1024)}, f32[2048]{0:T(1024)S(1)}, u32[]{:S(2)}) copy-start(f32[2048]{0:T(1024)S(1)} %fusion.80) | copy-start | bytes 24580
  269.0 17.5 %copy-start.18 = (f32[2048]{0:T(1024)S(1)}, f32[2048]{0:T(1024)}, u32[]{:S(2)}) copy-start(f32[2048]{0:T(1024)} %copy-done.17) | copy-start | bytes 24580
  269.0 17.6 %copy-start = (bf16[1,2048,1024]{1,2,0:T(8,128)(2,1)S(1)}, bf16[1,2048,1024]{1,2,0:T(8,128)(2,1)}, u32[]{:S(2)}) copy-start(bf16[1,2048,1024]{1,2,0:T(8,128)(2,1)} %copy.21) | copy-start | bytes 12582916
  269.0 17.6 %copy-start.5 = (bf16[2048,1024]{0,1:T(8,128)(2,1)S(1)}, bf16[2048,1024]{0,1:T(8,128)(2,1)}, u32[]{:S(2)}) copy-start(bf16[2048,1024]{0,1:T(8,128)(2,1)} %get-tuple-element.27) | copy-start | bytes 12582916
  308.1 122.2 %reduce-scatter.17.cloned.1.call-start = ((), (), s32[]{:S(2)}) async-start(), calls=%async_computation.11 | async-start | bytes 5898240 | tf_op jit(solution)/shard_map/reduce_scatter | solution.py:53
  330.2 17.3 %copy-start.20 = (f32[2048]{0:T(1024)S(1)}, f32[2048]{0:T(1024)}, u32[]{:S(2)}) copy-start(f32[2048]{0:T(1024)} %copy-done.19) | copy-start | bytes 24580
  330.2 102.8 %reduce-scatter.11.cloned.1.call-start = ((), (), s32[]{:S(2)}) async-start(), calls=%async_computation.8 | async-start | bytes 5898240 | tf_op jit(solution)/shard_map/reduce_scatter | solution.py:53
  367.5 86.7 %reduce-scatter.13.cloned.1.call-start = ((), (), s32[]{:S(2)}) async-start(), calls=%async_computation.9 | async-start | bytes 5898240 | tf_op jit(solution)/shard_map/reduce_scatter | solution.py:53
  388.4 103.5 %reduce-scatter.7.cloned.1.call-start = ((), (), s32[]{:S(2)}) async-start(), calls=%async_computation.6 | async-start | bytes 5898240 | tf_op jit(solution)/shard_map/reduce_scatter | solution.py:53
  413.3 116.1 %reduce-scatter.9.cloned.1.call-start = ((), (), s32[]{:S(2)}) async-start(), calls=%async_computation.7 | async-start | bytes 5898240 | tf_op jit(solution)/shard_map/reduce_scatter | solution.py:53
  430.2 120.1 %copy-start.2 = (bf16[2,320,1024]{2,1,0:T(8,128)(2,1)S(1)}, bf16[2,320,1024]{2,1,0:T(8,128)(2,1)}, u32[]{:S(2)}) copy-start(bf16[2,320,1024]{2,1,0:T(8,128)(2,1)} %param.15) | copy-start | bytes 3932164
  529.4 27.1 %copy-start.13 = (bf16[128,2560]{1,0:T(8,128)(2,1)S(1)}, bf16[128,2560]{1,0:T(8,128)(2,1)}, u32[]{:S(2)}) copy-start(bf16[128,2560]{1,0:T(8,128)(2,1)} %reduce-scatter.7.cloned.1.call-done) | copy-start | bytes 1966084
  529.4 27.1 %copy-start.14 = (bf16[128,2560]{1,0:T(8,128)(2,1)S(1)}, bf16[128,2560]{1,0:T(8,128)(2,1)}, u32[]{:S(2)}) copy-start(bf16[128,2560]{1,0:T(8,128)(2,1)} %reduce-scatter.9.cloned.1.call-done) | copy-start | bytes 1966084
  550.4 9.0 %copy-start.10 = (f32[2,128,2560]{2,1,0:T(8,128)S(1)}, f32[2,128,2560]{2,1,0:T(8,128)}, u32[]{:S(2)}) copy-start(f32[2,128,2560]{2,1,0:T(8,128)} %param.17) | copy-start | bytes 7864324
  550.4 9.1 %copy-start.11 = (bf16[128,2560]{1,0:T(8,128)(2,1)S(1)}, bf16[128,2560]{1,0:T(8,128)(2,1)}, u32[]{:S(2)}) copy-start(bf16[128,2560]{1,0:T(8,128)(2,1)} %reduce-scatter.11.cloned.1.call-done) | copy-start | bytes 1966084
  550.4 9.3 %copy-start.12 = (bf16[128,2560]{1,0:T(8,128)(2,1)S(1)}, bf16[128,2560]{1,0:T(8,128)(2,1)}, u32[]{:S(2)}) copy-start(bf16[128,2560]{1,0:T(8,128)(2,1)} %reduce-scatter.13.cloned.1.call-done) | copy-start | bytes 1966084
  (9 other events, 43.1 us)
Sparse Core Ops, SparseCore 0:
  10.2 35.3 all-gather.12
  47.7 32.1 all-gather.14
  82.1 32.1 all-gather.16
  116.3 32.1 all-gather.20
  150.5 32.1 all-gather.22
  184.7 32.1 all-gather.18
  308.2 33.1 reduce-scatter.14
  343.6 35.3 reduce-scatter.16
  381.3 35.3 reduce-scatter.10
  418.9 35.3 reduce-scatter.12
  456.5 35.3 reduce-scatter.6
  494.1 35.3 reduce-scatter.8
where the time goes:
time: 581 us; the launch traced here: 573 us
  matrix products  307 us (53%)
  waiting for transfers between devices  180 us (31%)
  other arithmetic  26.9 us (5%)
  local copies, waits for them, and re-layouts  25.4 us (4%)
  between operations  17.6 us (3%)
  blocking collectives  15.6 us (3%)
    dot_general x5, matrix products, layer(): gate = jnp.dot(a, w['w_gate'], preferred_element_type=jnp.float32)  110 us
    dot_general x5, matrix products, layer(): up = jnp.dot(a, w['w_up'], preferred_element_type=jnp.float32)  107 us
    reduce_scatter x6, waiting for transfers between devices, step(): lax.psum_scatter(by_w[name], 'dp', scatter_dimension=0, tiled=True)  93.9 us
    dot_general x5, matrix products, matmul(): jnp.dot(a, w, preferred_element_type=jnp.float32).astype(jnp.bfloat16)  90 us
    all_gather x6, waiting for transfers between devices, fetched(): lax.all_gather(w[number], 'dp', axis=0, tiled=True)  84.2 us
    unnamed x44, local copies, waits for them, and re-layouts  19.3 us
    psum x1, blocking collectives, step(): squares = lax.psum(sum((jnp.sum(g * g) for g in gradients)), 'dp')  15.6 us
    convert_element_type x2, other arithmetic, adamw(): return ((w - 0.02 * step).astype(jnp.bfloat16), m, v)  12.3 us
  transfers between devices with their start and end apart: 12, of which 9 were waited for; matrix products, arithmetic and copies ran while one was open for 43% of the time, Pallas kernels for 0%

commit v1 on v0

v1 whole, which is shorter than its diff:
```python
import functools

import jax
import jax.numpy as jnp
from jax import lax
from jax.experimental import pallas as pl
from jax.experimental.pallas import tpu as pltpu
from jax.sharding import PartitionSpec as P

MESH = pl.DeviceIdType.MESH
ANY = pl.BlockSpec(memory_space=pl.ANY)
F32, BF16 = jnp.float32, jnp.bfloat16
LANES = 128
NT = (((1,), (1,)), ((), ()))
TN = (((0,), (0,)), ((), ()))


def places(n):
    me = lax.axis_index("dp")
    core, chips = lax.rem(me, 2), n // 2
    chip = me // 2
    around = lambda k: lax.rem(chip + k, chips) * 2 + core
    return me, chip, core, me + 1 - 2 * core, around(1), around(chips - 1), around(2)


def greet(*others):
    barrier = pltpu.get_barrier_semaphore()
    for other in others:
        pl.semaphore_signal(barrier, inc=1, device_id={"dp": other}, device_id_type=MESH)
    pl.semaphore_wait(barrier, len(others))


def norm_rows(wide):
    scale = lax.rsqrt(jnp.mean(wide * wide, -1, keepdims=True) + 1e-6)
    return (wide * scale).astype(BF16)


def forward_kernel(n, x_ref, wg_ref, wu_ref, wd_ref, g_ref, u_ref, d_ref, a_out, h_out, gate_out, up_out,
                   own_g, own_u, own_d, h, a, hidden, wchunk, wdown, stage,
                   send, recv, own_sem, out_sem, w_sem, stage_sem, misc):
    me, chip, core, partner, right, left, far = places(n)
    layers = wg_ref.shape[0]
    tokens, d = x_ref.shape
    chunks, _, width = gate_out.shape[1:]
    chips = n // 2
    tile = stage.shape[2]
    tiles = tokens // tile
    span = g_ref.shape[2] // chips

    order = [(l, w, o) for l in range(layers) for w, o in ((g_ref, own_g), (u_ref, own_u), (d_ref, own_d))]

    loads = [pltpu.make_async_copy(src.at[l], o.at[l], own_sem.at[3 * l + i])
             for l in range(layers) for i, (src, o) in enumerate(((wg_ref, own_g), (wu_ref, own_u), (wd_ref, own_d)))]
    for one in loads:
        one.start()
    load_x = pltpu.make_async_copy(x_ref, h, misc.at[0])
    load_x.start()
    greet(partner, right, left)

    def rows(m, device, part=None):
        l, w, o = order[m]
        count = o.shape[1]
        if part is None:
            return w.at[l, pl.ds(device * count, count)]
        return w.at[l, pl.ds(device * count + part * (count // 2), count // 2)]

    def ag(m, kind):
        l, w, o = order[m]
        src, to = [
            (None, right), (None, left),
            (rows(m, left, 0), right), (rows(m, right, 1), left),
            (None, partner), (rows(m, left), partner), (rows(m, right), partner),
            (rows(m, far, 0), partner), (rows(m, far, 1), partner),
        ][kind]
        dst = rows(m, me) if src is None else src
        return pltpu.make_async_remote_copy(o.at[l] if src is None else src, dst, send.at[m, kind], recv.at[m, kind],
                                            device_id={"dp": to}, device_id_type=MESH)

    kept = []

    def begin(m):
        loads[m].wait()
        ag(m, 0).start()
        ag(m, 1).start()
        ag(m, 4).start()
        l, w, o = order[m]
        copy = pltpu.make_async_copy(o.at[l], rows(m, me), out_sem.at[m])
        copy.start()
        kept.append(copy)

    def pass_on(m):
        ag(m, 0).wait_recv()
        ag(m, 2).start()
        ag(m, 5).start()
        ag(m, 1).wait_recv()
        ag(m, 3).start()
        ag(m, 6).start()

    def hand_over(m):
        ag(m, 2).wait_recv()
        ag(m, 7).start()
        ag(m, 3).wait_recv()
        ag(m, 8).start()

    def complete(m):
        for kind in (4, 5, 6, 7, 8):
            ag(m, kind).wait_recv()
        kept[m].wait()

    begin(0)
    begin(1)
    load_x.wait()

    def norm_step(t, _):
        r = pl.ds(pl.multiple_of(t * 256, 256), 256)
        a[r, :] = norm_rows(h[r, :].astype(F32))
        return 0
    lax.fori_loop(0, tokens // 256, norm_step, 0)
    a_copy = pltpu.make_async_copy(a, a_out.at[0], misc.at[1])
    a_copy.start()

    def w_loads(l, j, slot):
        return [pltpu.make_async_copy(w.at[l, :, pl.ds(c * span + j * LANES, LANES)], wchunk.at[slot, i, :, pl.ds(c * LANES, LANES)],
                                      w_sem.at[slot, i, c])
                for i, w in enumerate((g_ref, u_ref)) for c in range(chips)]

    def gate_up(l, between, with_hidden):
        for one in w_loads(l, 0, 0):
            one.start()
        for j in range(chunks):
            slot = j % 2
            for one in w_loads(l, j, slot):
                one.wait()
            if j + 1 < chunks:
                for one in w_loads(l, j + 1, 1 - slot):
                    one.start()

            def step(t, _):
                half = lax.rem(t, 2)
                r = pl.ds(pl.multiple_of(t * tile, tile), tile)

                def outs(t_):
                    rr = pl.ds(pl.multiple_of(t_ * tile, tile), tile)
                    hh = lax.rem(t_, 2)
                    return [pltpu.make_async_copy(stage.at[hh, i], o.at[l, j, rr], stage_sem.at[hh, i])
                            for i, o in enumerate((gate_out, up_out))]

                @pl.when(t >= (2 if j == 0 else 0))
                def _():
                    for one in outs(t):
                        one.wait()
                rows_a = a[r, :]
                stage[half, 0] = jnp.dot(rows_a, wchunk[slot, 0], preferred_element_type=F32)
                stage[half, 1] = jnp.dot(rows_a, wchunk[slot, 1], preferred_element_type=F32)
                if with_hidden:
                    gate, up = stage[half, 0], stage[half, 1]
                    hidden[r, pl.ds(j * width, width)] = (jax.nn.silu(gate) * up).astype(BF16)
                for one in outs(t):
                    one.start()
                return 0
            lax.fori_loop(0, tiles, step, 0)
            between(j)
        for half in range(2):
            for i, o in enumerate((gate_out, up_out)):
                pltpu.make_async_copy(stage.at[half, i], o.at[l, 0, pl.ds(0, tile)], stage_sem.at[half, i]).wait()

    pass_on(0)
    pass_on(1)
    begin(2)
    begin(3)
    hand_over(0)
    hand_over(1)
    complete(0)
    complete(1)

    def first(j):
        if j == 2:
            pass_on(2)
            begin(4)
        if j == 4:
            pass_on(3)
    gate_up(0, first, True)

    hand_over(2)
    complete(2)
    down = [pltpu.make_async_copy(d_ref.at[0, pl.ds(c * span + j * LANES, LANES)], wdown.at[pl.ds(j * width + c * LANES, LANES)], misc.at[3 + j * chips + c])
            for j in range(chunks) for c in range(chips)]
    for one in down:
        one.start()
    a_copy.wait()
    for one in down:
        one.wait()

    def down_step(t, _):
        r = pl.ds(pl.multiple_of(t * tile, tile), tile)
        y = jnp.dot(hidden[r, :], wdown[...], preferred_element_type=F32).astype(BF16)
        h1 = (h[r, :].astype(F32) + y.astype(F32)).astype(BF16)
        h[r, :] = h1
        a[r, :] = norm_rows(h1.astype(F32))
        return 0
    lax.fori_loop(0, tiles, down_step, 0)
    h_copy = pltpu.make_async_copy(h, h_out, misc.at[2])
    h_copy.start()
    a_copy = pltpu.make_async_copy(a, a_out.at[1], misc.at[1])
    a_copy.start()
    pass_on(4)
    begin(5)
    hand_over(3)
    hand_over(4)
    complete(3)
    complete(4)

    def second(j):
        if j == 2:
            pass_on(5)
    gate_up(1, second, False)
    hand_over(5)
    complete(5)
    h_copy.wait()
    a_copy.wait()
    for m in range(len(order)):
        for kind in range(9):
            ag(m, kind).wait_send()


def forward(n, x, wg, wu, wd):
    tokens, d = x.shape
    layers, _, ff = wg.shape
    chips = n // 2
    width = chips * LANES
    chunks = ff // width
    tile = 512
    sds = jax.ShapeDtypeStruct
    dma = pltpu.SemaphoreType.DMA
    return pl.pallas_call(
        functools.partial(forward_kernel, n),
        name="forward",
        out_shape=(
            sds((layers, d, ff), BF16), sds((layers, d, ff), BF16), sds((layers, ff, d), BF16),
            sds((layers, tokens, d), BF16), sds((tokens, d), BF16),
            sds((layers, chunks, tokens, width), F32), sds((layers, chunks, tokens, width), F32),
        ),
        in_specs=[ANY] * 4,
        out_specs=(ANY,) * 7,
        scratch_shapes=[
            pltpu.VMEM(wg.shape, BF16), pltpu.VMEM(wu.shape, BF16), pltpu.VMEM(wd.shape, BF16),
            pltpu.VMEM((tokens, d), BF16), pltpu.VMEM((tokens, d), BF16), pltpu.VMEM((tokens, ff), BF16),
            pltpu.VMEM((2, 2, d, width), BF16), pltpu.VMEM((ff, d), BF16), pltpu.VMEM((2, 2, tile, width), F32),
            dma((3 * layers, 9)), dma((3 * layers, 9)), dma((3 * layers,)), dma((3 * layers,)),
            dma((2, 2, chips)), dma((2, 2)), dma((3 + chunks * chips,)),
        ],
        compiler_params=pltpu.CompilerParams(collective_id=0, has_side_effects=True, vmem_limit_bytes=60 * 1024 * 1024),
    )(x, wg, wu, wd)


SLOTS = 4


def backward_kernel(n, dy_ref, g_ref, u_ref, d_ref, a_ref, h_ref, gate_ref, up_ref, gg_out, gu_out, gd_out, sq_out,
                    ct, at, nat, da, hid, hid_t, dg, du, dh, stage, wd, wgu, own, out_p, in_p, out_1, in_1, out_2, in_2, fin,
                    gg, gu, gd, sq, squares,
                    stage_sem, wd_sem, wgu_sem, p_send, p_recv, s1_send, s1_recv, s2_send, s2_recv, f_send, f_recv, q_send, q_recv, misc):
    me, chip, core, partner, right, left, far = places(n)
    layers, chunks, tokens, width = gate_ref.shape
    d = dy_ref.shape[1]
    chips = n // 2
    span = g_ref.shape[2] // chips
    share = gd.shape[1]
    tile = stage.shape[2]
    tiles = tokens // tile
    sub = 256
    total = layers * chunks
    half = d // 2

    def layer_of(jj):
        return layers - 1 - jj // chunks

    def stage_loads(s):
        jj, t = s // tiles, lax.rem(s, tiles)
        slot = lax.rem(s, 2)
        r = pl.ds(pl.multiple_of(t * tile, tile), tile)
        return [pltpu.make_async_copy(ref.at[layer_of(jj), lax.rem(jj, chunks), r], stage.at[slot, i], stage_sem.at[slot, i])
                for i, ref in enumerate((gate_ref, up_ref))]

    def wd_loads(jj):
        l, j, slot = layer_of(jj), lax.rem(jj, chunks), lax.rem(jj, 2)
        return [pltpu.make_async_copy(d_ref.at[l, pl.ds(pl.multiple_of(c * span + j * LANES, LANES), LANES)],
                                      wd.at[slot, pl.ds(c * LANES, LANES)], wd_sem.at[slot, c]) for c in range(chips)]

    def wgu_loads(jj):
        l, j, slot = layer_of(jj), lax.rem(jj, chunks), lax.rem(jj, 2)
        return [pltpu.make_async_copy(ref.at[l, :, pl.ds(pl.multiple_of(c * span + j * LANES, LANES), LANES)],
                                      wgu.at[slot, i, :, pl.ds(c * LANES, LANES)], wgu_sem.at[slot, i, c])
                for i, ref in enumerate((g_ref, u_ref)) for c in range(chips)]

    first = [pltpu.make_async_copy(a_ref.at[layers - 1], nat, misc.at[0]), pltpu.make_async_copy(dy_ref, ct, misc.at[1])]
    for one in first + stage_loads(0) + wd_loads(0) + wgu_loads(0):
        one.start()

    barrier = pltpu.get_barrier_semaphore()
    others = [lax.rem(me + k, n) for k in range(1, n)]
    for other in others:
        pl.semaphore_signal(barrier, inc=1, device_id={"dp": other}, device_id_type=MESH)
    pl.semaphore_wait(barrier, n - 1)

    def zero(t, _):
        da[pl.ds(pl.multiple_of(t * 128, 128), 128), :] = jnp.zeros((128, d), F32)
        return 0
    lax.fori_loop(0, tokens // 128, zero, 0)
    sq[...] = jnp.zeros_like(sq)

    def turn(t, _):
        r = pl.ds(pl.multiple_of(t * sub, sub), sub)
        for c in range(chips):
            for hh in range(2):
                piece = nat[r, pl.ds((2 * c + hh) * LANES, LANES)]
                at[pl.ds(hh * half + c * LANES, LANES), r] = piece.T
        return 0

    for one in first:
        one.wait()
    lax.fori_loop(0, tokens // sub, turn, 0)
    load_h = pltpu.make_async_copy(h_ref, nat, misc.at[0])
    load_h.start()

    def remote(src, dst, ss, rs, to):
        return pltpu.make_async_remote_copy(src, dst, ss, rs, device_id={"dp": to}, device_id_type=MESH)

    def p_copy(k):
        s = lax.rem(k, SLOTS)
        return remote(out_p.at[s], in_p.at[s], p_send.at[s], p_recv.at[s], partner)

    def s1_copy(k, way):
        s = lax.rem(k, SLOTS)
        return remote(out_1.at[s, way], in_1.at[s, way], s1_send.at[s, way], s1_recv.at[s, way], (right, left)[way])

    def s2_copy(k, way):
        s = lax.rem(k, SLOTS)
        return remote(out_2.at[s, way], in_2.at[s, way], s2_send.at[s, way], s2_recv.at[s, way], (right, left)[way])

    mid = LANES // 2
    block_r, block_l, block_f = (lax.rem(chip + k, chips) for k in (1, chips - 1, 2))

    def pair_step(k):
        s = lax.rem(k, SLOTS)
        p_copy(k).wait_recv()

        @pl.when(k >= SLOTS)
        def _():
            s1_copy(k - SLOTS, 0).wait_send()
            s1_copy(k - SLOTS, 1).wait_send()
        for way in range(2):
            rows = pl.ds(way * mid, mid)
            out_1[s, way] = (own[s, block_f, rows, :] + in_p[s, block_f, rows, :].astype(F32)).astype(BF16)
        s1_copy(k, 0).start()
        s1_copy(k, 1).start()
        for block in (block_r, block_l, chip):
            own[s, block] += in_p[s, block].astype(F32)

    def pass_step(k):
        s = lax.rem(k, SLOTS)
        s1_copy(k, 0).wait_recv()
        s1_copy(k, 1).wait_recv()

        @pl.when(k >= SLOTS)
        def _():
            s2_copy(k - SLOTS, 0).wait_send()
            s2_copy(k - SLOTS, 1).wait_send()
        for way, block in ((0, block_r), (1, block_l)):
            for part in range(2):
                rows = pl.ds(part * mid, mid)
                value = own[s, block, rows, :]
                if part == way:
                    value = value + in_1[s, way].astype(F32)
                out_2[s, way, rows, :] = value.astype(BF16)
        s2_copy(k, 0).start()
        s2_copy(k, 1).start()

    def f_copy(l, j, part):
        row = j * LANES + core * mid
        row = row - (row // share) * share
        rows = pl.ds(pl.multiple_of(row, mid), mid)
        return remote(fin.at[l, j, pl.ds(part * mid, mid)], gd.at[l, rows, pl.ds(part * width, width)],
                      f_send.at[l, j, part], f_recv.at[l, j, part], partner)

    def final_step(k, kind):
        s = lax.rem(k, SLOTS)
        jj = k // 3
        l, j = layer_of(jj), lax.rem(jj, chunks)
        s2_copy(k, 0).wait_recv()
        s2_copy(k, 1).wait_recv()
        value = own[s, chip] + in_2[s, 0].astype(F32) + in_2[s, 1].astype(F32)
        value = value.astype(BF16)
        wide = value.astype(F32)
        sq[...] += jnp.sum((wide * wide).reshape(LANES // 8, 8, width), 0)
        if kind:
            to = gg if kind == 1 else gu
            for c in range(chips):
                to[l, :, pl.ds(pl.multiple_of(c * span + j * LANES, LANES), LANES)] = value[:, c * LANES:(c + 1) * LANES]
        else:
            row = j * LANES + core * mid
            owner = row // share
            local = pl.multiple_of(row - owner * share, mid)

            @pl.when(owner == core)
            def _():
                for part in range(2):
                    gd[l, pl.ds(local, mid), pl.ds(part * width, width)] = value[part * mid:(part + 1) * mid, :]

            @pl.when(owner != core)
            def _():
                fin[l, j] = value
                f_copy(l, j, 0).start()
                f_copy(l, j, 1).start()

    def store(kind, ref, s, value):
        if kind:
            for c in range(chips):
                ref[s, c] = value[c * LANES:(c + 1) * LANES, :].astype(ref.dtype)
        else:
            for c in range(chips):
                for part in range(2):
                    ref[s, c, pl.ds(part * mid, mid), :] = value[c * mid:(c + 1) * mid, part * width:(part + 1) * width].astype(ref.dtype)

    def product(kind, which):
        if kind == 0:
            rows = pl.ds(pl.multiple_of(which * (width // 2), width // 2), width // 2)
            return jnp.dot(hid_t[rows, :], ct[...], preferred_element_type=F32)
        rows = pl.ds(pl.multiple_of(which * half, half), half)
        return jnp.dot(at[rows, :], (dg if kind == 1 else du)[...], preferred_element_type=F32)

    def tick(k, kind, maybe):
        s = lax.rem(k, SLOTS)

        @pl.when(k >= SLOTS)
        def _():
            p_copy(k - SLOTS).wait_send()
        store(kind, out_p, s, product(kind, 1 - core))
        p_copy(k).start()
        store(kind, own, s, product(kind, core))

        def run(step, lag, *more):
            if maybe and lag > kind:
                pl.when(k >= lag)(lambda: step(k - lag, *more))
            else:
                step(k - lag, *more)
        run(pair_step, 1)
        run(pass_step, 2)
        run(final_step, 3, kind)

    def chunk(jj, _):
        l, slot = layer_of(jj), lax.rem(jj, 2)

        @pl.when(jj == chunks)
        def _():
            load_h.wait()

            def to_h(t, _):
                r = pl.ds(pl.multiple_of(t * 128, 128), 128)
                wide = nat[r, :].astype(F32)
                grad = da[r, :]
                scale = lax.rsqrt(jnp.mean(wide * wide, -1, keepdims=True) + 1e-6)
                back = grad * scale - wide * (scale * scale * scale * jnp.mean(grad * wide, -1, keepdims=True))
                ct[r, :] = (ct[r, :].astype(F32) + back.astype(BF16).astype(F32)).astype(BF16)
                return 0
            lax.fori_loop(0, tokens // 128, to_h, 0)
            load_a = pltpu.make_async_copy(a_ref.at[0], nat, misc.at[0])
            load_a.start()
            load_a.wait()
            lax.fori_loop(0, tokens // sub, turn, 0)

        for one in wd_loads(jj):
            one.wait()

        @pl.when(jj < chunks)
        def _():
            for one in wgu_loads(jj):
                one.wait()

        @pl.when(jj + 1 < total)
        def _():
            for one in wd_loads(jj + 1):
                one.start()

        @pl.when(jj + 1 < chunks)
        def _():
            for one in wgu_loads(jj + 1):
                one.start()

        def step(t, _):
            s = jj * tiles + t
            st = lax.rem(s, 2)
            for one in stage_loads(s):
                one.wait()

            @pl.when(s + 1 < total * tiles)
            def _():
                for one in stage_loads(s + 1):
                    one.start()
            for q in range(tile // sub):
                r = pl.ds(pl.multiple_of(t * tile + q * sub, sub), sub)
                dh[q] = lax.dot_general(ct[r, :], wd[slot], NT, preferred_element_type=F32)
                for e in range(sub // 32):
                    here = pl.ds(q * sub + e * 32, 32)
                    there = pl.ds(pl.multiple_of(t * tile + q * sub + e * 32, 32), 32)
                    gate, up = stage[st, 0, here, :], stage[st, 1, here, :]
                    back = dh[q, pl.ds(e * 32, 32), :].astype(BF16).astype(F32)
                    sig = jax.nn.sigmoid(gate)
                    silu = gate * sig
                    hid[there, :] = (silu * up).astype(BF16)
                    du[there, :] = (back * silu).astype(BF16)
                    dg[there, :] = (back * up * (sig + silu * (1.0 - sig))).astype(BF16)
                turned = hid[r, :].T
                for c in range(chips):
                    for hh in range(2):
                        hid_t[pl.ds(hh * (width // 2) + c * mid, mid), r] = turned[c * LANES + hh * mid:c * LANES + (hh + 1) * mid, :]
            return 0
        lax.fori_loop(0, tiles, step, 0)

        @pl.when(jj < chunks)
        def _():
            def back_step(t, _):
                r = pl.ds(pl.multiple_of(t * tile, tile), tile)
                da[r, :] += (lax.dot_general(dg[r, :], wgu[slot, 0], NT, preferred_element_type=F32)
                             + lax.dot_general(du[r, :], wgu[slot, 1], NT, preferred_element_type=F32))
                return 0
            lax.fori_loop(0, tiles, back_step, 0)

        for kind in range(3):
            tick(jj * 3 + kind, kind, True)
        return 0
    lax.fori_loop(0, total, chunk, 0)

    last = 3 * total
    pair_step(last - 1)
    pass_step(last - 2)
    final_step(last - 3, 0)
    pass_step(last - 1)
    final_step(last - 2, 1)
    final_step(last - 1, 2)

    squares[me] = jnp.sum(sq[...].reshape(8, width // LANES, LANES), 1)
    copies = [remote(squares.at[me], squares.at[me], q_send.at[k], q_recv.at[k], other) for k, other in enumerate(others)]
    for one in copies:
        one.start()
    outs = [pltpu.make_async_copy(a, b, misc.at[2 + i]) for i, (a, b) in enumerate(((gg, gg_out), (gu, gu_out)))]
    for one in outs:
        one.start()
    for l in range(layers):
        for j in range(chunks):
            row = j * LANES + core * mid

            @pl.when(row // share != core)
            def _():
                f_copy(l, j, 0).wait_send()
                f_copy(l, j, 1).wait_send()
            row = j * LANES + (1 - core) * mid

            @pl.when(row // share == core)
            def _():
                @pl.when(row // share != 1 - core)
                def _():
                    f_copy(l, j, 0).wait_recv()
                    f_copy(l, j, 1).wait_recv()
    outs.append(pltpu.make_async_copy(gd, gd_out, misc.at[4]))
    outs[-1].start()
    for one in copies:
        one.wait_recv()
    whole = squares[0]
    for k in range(1, n):
        whole = whole + squares[k]
    squares[n] = jnp.broadcast_to(jnp.sum(whole), (8, LANES))
    outs.append(pltpu.make_async_copy(squares.at[n], sq_out, misc.at[5]))
    outs[-1].start()
    for k in range(last - SLOTS, last):
        p_copy(k).wait_send()
        for way in range(2):
            s1_copy(k, way).wait_send()
            s2_copy(k, way).wait_send()
    for one in copies:
        one.wait_send()
    for one in outs:
        one.wait()


def backward(n, dy, g, u, dn, a, h, gate, up):
    tokens, d = dy.shape
    layers, chunks, _, width = gate.shape
    ff = g.shape[2]
    chips = n // 2
    tile = 512
    sds = jax.ShapeDtypeStruct
    dma = pltpu.SemaphoreType.DMA
    v = pltpu.VMEM
    mid = LANES // 2
    grads = [((layers, d // n, ff), BF16), ((layers, d // n, ff), BF16), ((layers, ff // n, d), BF16)]
    return pl.pallas_call(
        functools.partial(backward_kernel, n),
        name="backward",
        out_shape=tuple(sds(*g_) for g_ in grads) + (sds((8, LANES), F32),),
        in_specs=[ANY] * 8,
        out_specs=(ANY,) * 4,
        scratch_shapes=[
            v((tokens, d), BF16), v((d, tokens), BF16), v((tokens, d), BF16), v((tokens, d), F32),
            v((tokens, width), BF16), v((width, tokens), BF16), v((tokens, width), BF16), v((tokens, width), BF16),
            v((tile // 256, 256, width), F32), v((2, 2, tile, width), F32), v((2, width, d), BF16), v((2, 2, d, width), BF16),
            v((SLOTS, chips, LANES, width), F32), v((SLOTS, chips, LANES, width), BF16), v((SLOTS, chips, LANES, width), BF16),
            v((SLOTS, 2, mid, width), BF16), v((SLOTS, 2, mid, width), BF16),
            v((SLOTS, 2, LANES, width), BF16), v((SLOTS, 2, LANES, width), BF16),
            v((layers, chunks, LANES, width), BF16),
            *(v(*g_) for g_ in grads), v((8, width), F32), v((n + 1, 8, LANES), F32),
            dma((2, 2)), dma((2, chips)), dma((2, 2, chips)), dma((SLOTS,)), dma((SLOTS,)),
            dma((SLOTS, 2)), dma((SLOTS, 2)), dma((SLOTS, 2)), dma((SLOTS, 2)),
            dma((layers, chunks, 2)), dma((layers, chunks, 2)), dma((n - 1,)), dma((n - 1,)), dma((6,)),
        ],
        compiler_params=pltpu.CompilerParams(collective_id=1, has_side_effects=True, vmem_limit_bytes=60 * 1024 * 1024),
    )(dy, g, u, dn, a, h, gate, up)


def adamw(w, m, v, g):
    m = 0.9 * m + 0.1 * g
    v = 0.95 * v + 0.05 * g * g
    step = m * lax.rsqrt(v + 1e-8) + 0.1 * w
    return (w - 0.02 * step).astype(BF16), m, v


def solution(mesh):
    n = mesh.shape["dp"]

    def step(x, dy, *arrays):
        weights, m, v = (arrays[i : i + 3] for i in (0, 3, 6))
        g, u, dn, a, h, gate, up = forward(n, x[0], *weights)
        *gradients, squares = backward(n, dy[0], g, u, dn, a, h, gate, up)
        factor = jnp.minimum(1.0, 0.5 * lax.rsqrt(squares[0, 0] / (n * sum(w.size for w in weights)) + 1e-30))
        new = [adamw(w.astype(F32), m, v, g.astype(F32) * factor) for w, m, v, g in zip(weights, m, v, gradients, strict=True)]
        return tuple(one[which] for which in range(3) for one in new)

    states, cut = P(("rep", "dp"), None, None), P(None, "dp", None)
    return jax.shard_map(
        step,
        mesh=mesh,
        in_specs=(states, states) + (cut,) * 9,
        out_specs=(P("rep", "dp", None),) * 9,
        check_vma=False,
    )
```

time: 581 us -> 423 us (0.73); the launches traced: 573 us -> 422 us
  Pallas kernels: 0 us -> 404 us
  matrix products: 307 us -> 0 us
  waiting for transfers between devices: 180 us -> 0 us
  local copies, waits for them, and re-layouts: 25.4 us -> 3.43 us
  between operations: 17.6 us -> 1.45 us
  blocking collectives: 15.6 us -> 0 us
  other arithmetic: 26.9 us -> 13 us
    pallas_call x0 -> x2, Pallas kernels: none -> 404 us  [the longest x1 257 us: backward(): pl.pallas_call(functools.partial(backward_kernel, n), name='backward', ou...]
    dot_general x15 -> x0, matrix products: 307 us -> none  [the longest x5 110 us: layer(): gate = jnp.dot(a, w['w_gate'], preferred_element_type=jnp.float32)]
    reduce_scatter x6 -> x0, waiting for transfers between devices: 93.9 us -> none  [step(): lax.psum_scatter(by_w[name], 'dp', scatter_dimension=0, tiled=True)]
    all_gather x6 -> x0, waiting for transfers between devices: 84.2 us -> none  [fetched(): lax.all_gather(w[number], 'dp', axis=0, tiled=True)]
    unnamed x44 -> x18, local copies, waits for them, and re-layouts: 19.3 us -> 2.24 us
    psum x1 -> x0, blocking collectives: 15.6 us -> none  [step(): squares = lax.psum(sum((jnp.sum(g * g) for g in gradients)), 'dp')]
    reduce_sum x4 -> x0, other arithmetic: 10.9 us -> none  [the longest x3 7.88 us: step(): squares = lax.psum(sum((jnp.sum(g * g) for g in gradients)), 'dp')]
  transfers between devices with their start and end apart: 12 -> 0, of which waited for: 9 -> 0; matrix products, arithmetic and copies ran while one was open for 43% -> 0% of each run, Pallas kernels for 0% -> 0%
where the time goes in v1:
time: 423 us; the launch traced here: 422 us
  Pallas kernels  404 us (96%)
  other arithmetic  13 us (3%)
    pallas_call x1, Pallas kernels, backward(): pl.pallas_call(functools.partial(backward_kernel, n), name='backward', ou...  257 us
    pallas_call x1, Pallas kernels, forward(): pl.pallas_call(functools.partial(forward_kernel, n), name='forward', out_...  147 us
    convert_element_type x2, other arithmetic, adamw(): return ((w - 0.02 * step).astype(BF16), m, v)  13 us

profile of v1, /device:TPU:113, one launch (start us, length us, event | category | flops | bytes accessed | tf_op | source)
XLA Modules:
  0.0 421.7 jit_solution(4657463890530698986)
XLA Ops:
  0.6 146.8 %forward.1 = (bf16[2,1024,2560]{2,1,0:T(8,128)(2,1)}, bf16[2,1024,2560]{2,1,0:T(8,128)(2,1)}, bf16[2,2560,1024]{2,1,0:T(8,128)(2,1)}, bf16[2,2048,1024]{2,1,0:T(...) custom-call(bf16[2048,1024]{1,0:T(8,128)(2,1)} %bitcast.4, ...), custom_call_target="tpu_custom_call" | custom-call | tf_op jit(solution)/shard_map/forward/pallas_call | solution.py:235
  147.5 0.0 copy-start
  147.5 0.0 copy-start.3
  147.5 257.0 %backward.1 = (bf16[2,128,2560]{2,1,0:T(8,128)(2,1)}, bf16[2,128,2560]{2,1,0:T(8,128)(2,1)}, bf16[2,320,1024]{2,1,0:T(8,128)(2,1)}, f32[8,128]{1,0:T(8,128)}) custom-call(bf16[2048,1024]{1,0:T(8,128)(2,1)} %bitcast.3, bf16[2,1024,2560]{2,1,0:T(8,128)(2,1)} %get-tuple-element.20.g_ref, bf16[2,1024,2560]{2,1,0:T(8,128)(2,1)} %get-tuple-element.21.u_ref, ...), custom_call_target="tpu_custom_call" | custom-call | tf_op jit(solution)/shard_map/backward/pallas_call | solution.py:597
  404.6 1.2 slice.3
  406.4 0.0 copy-done
  406.5 0.0 copy-done.3
  406.5 0.0 copy-start.1
  406.5 0.0 copy-start.2
  406.5 0.0 copy-start.4
  406.5 0.0 copy-start.5
  406.5 0.0 copy-start.6
  406.5 0.0 copy-start.7
  406.5 0.0 copy-start.8
  406.5 6.4 %fusion.8 = (bf16[2,320,1024]{2,1,0:T(8,128)(2,1)}, f32[2,320,1024]{2,1,0:T(8,128)}, f32[2,320,1024]{2,1,0:T(8,128)}) fusion(bf16[2,320,1024]{2,1,0:T(8,128)(2,1)S(1)} %copy-done, f32[]{:T(128)} %bitcast.2, bf16[2,320,1024]{2,1,0:T(8,128)(2,1)} %get-tuple-element.30, f32[2,320,1024]{2,1,0:T(8,128)S(1)} %copy-done.3, f32[2,320,1024]{2,1,0:T(8,128)} %param.18), kind=kLoop, calls=%fused_computation.17 | loop fusion | flops 11141120 | bytes 14417924 | tf_op jit(solution)/shard_map/convert_element_type | solution.py:624
  412.9 0.0 copy-done.1
  412.9 0.0 copy-done.2
  412.9 0.0 copy-done.4
  412.9 0.0 copy-done.5
  412.9 1.1 copy-done.6
  414.1 0.7 copy-done.7
  414.8 0.3 copy-done.8
  415.1 6.6 %fusion.2 = (bf16[2,128,2560]{2,1,0:T(8,128)(2,1)}, f32[2,128,2560]{2,1,0:T(8,128)}, f32[2,128,2560]{2,1,0:T(8,128)}, bf16[2,128,2560]{2,1,0:T(8,128)(2,1)}, f32...) fusion(bf16[2,128,2560]{2,1,0:T(8,128)(2,1)S(1)} %copy-done.1, f32[]{:T(128)} %bitcast.2, ...), kind=kLoop, calls=%fused_computation.11 | loop fusion | flops 22282240 | bytes 28835844 | tf_op jit(solution)/shard_map/convert_element_type | solution.py:624
Async XLA Ops:
  147.5 259.0 %copy-start = (bf16[2,320,1024]{2,1,0:T(8,128)(2,1)S(1)}, bf16[2,320,1024]{2,1,0:T(8,128)(2,1)}, u32[]{:S(2)}) copy-start(bf16[2,320,1024]{2,1,0:T(8,128)(2,1)} %wd_ref.1) | copy-start | bytes 3932164
  147.5 259.0 %copy-start.3 = (f32[2,320,1024]{2,1,0:T(8,128)S(1)}, f32[2,320,1024]{2,1,0:T(8,128)}, u32[]{:S(2)}) copy-start(f32[2,320,1024]{2,1,0:T(8,128)} %param.21) | copy-start | bytes 7864324
  406.5 6.4 %copy-start.1 = (bf16[2,128,2560]{2,1,0:T(8,128)(2,1)S(1)}, bf16[2,128,2560]{2,1,0:T(8,128)(2,1)}, u32[]{:S(2)}) copy-start(bf16[2,128,2560]{2,1,0:T(8,128)(2,1)} %wg_ref.1) | copy-start | bytes 3932164
  406.5 6.4 %copy-start.2 = (bf16[2,128,2560]{2,1,0:T(8,128)(2,1)S(1)}, bf16[2,128,2560]{2,1,0:T(8,128)(2,1)}, u32[]{:S(2)}) copy-start(bf16[2,128,2560]{2,1,0:T(8,128)(2,1)} %wu_ref.1) | copy-start | bytes 3932164
  406.5 6.4 %copy-start.4 = (f32[2,128,2560]{2,1,0:T(8,128)S(1)}, f32[2,128,2560]{2,1,0:T(8,128)}, u32[]{:S(2)}) copy-start(f32[2,128,2560]{2,1,0:T(8,128)} %param.19) | copy-start | bytes 7864324
  406.5 6.4 %copy-start.5 = (f32[2,128,2560]{2,1,0:T(8,128)S(1)}, f32[2,128,2560]{2,1,0:T(8,128)}, u32[]{:S(2)}) copy-start(f32[2,128,2560]{2,1,0:T(8,128)} %param.16) | copy-start | bytes 7864324
  406.5 7.5 %copy-start.6 = (f32[2,128,2560]{2,1,0:T(8,128)S(1)}, f32[2,128,2560]{2,1,0:T(8,128)}, u32[]{:S(2)}) copy-start(f32[2,128,2560]{2,1,0:T(8,128)} %param.20) | copy-start | bytes 7864324
  406.5 8.3 %copy-start.7 = (f32[2,128,2560]{2,1,0:T(8,128)S(1)}, f32[2,128,2560]{2,1,0:T(8,128)}, u32[]{:S(2)}) copy-start(f32[2,128,2560]{2,1,0:T(8,128)} %param.17) | copy-start | bytes 7864324
  406.5 8.6 %copy-start.8 = (bf16[2,128,2560]{2,1,0:T(8,128)(2,1)S(1)}, bf16[2,128,2560]{2,1,0:T(8,128)(2,1)}, u32[]{:S(2)}) copy-start(bf16[2,128,2560]{2,1,0:T(8,128)(2,1)} %get-tuple-element.27) | copy-start | bytes 3932164

commit v2 on v1

--- a/solution.py
+++ b/solution.py
@@ -30,13 +30,17 @@
     pl.semaphore_wait(barrier, len(others))
 
 
+def sigmoid(x):
+    return 0.5 * jnp.tanh(0.5 * x) + 0.5
+
+
 def norm_rows(wide):
     scale = lax.rsqrt(jnp.mean(wide * wide, -1, keepdims=True) + 1e-6)
     return (wide * scale).astype(BF16)
 
 
 def forward_kernel(n, x_ref, wg_ref, wu_ref, wd_ref, g_ref, u_ref, d_ref, a_out, h_out, gate_out, up_out,
-                   own_g, own_u, own_d, h, a, hidden, wchunk, wdown, stage,
+                   own_g, own_u, own_d, h, a, at, hidden, wchunk, wdown, stage,
                    send, recv, own_sem, out_sem, w_sem, stage_sem, misc):
     me, chip, core, partner, right, left, far = places(n)
     layers = wg_ref.shape[0]
@@ -116,7 +120,15 @@
         a[r, :] = norm_rows(h[r, :].astype(F32))
         return 0
     lax.fori_loop(0, tokens // 256, norm_step, 0)
-    a_copy = pltpu.make_async_copy(a, a_out.at[0], misc.at[1])
+
+    def turn(t, _):
+        r = pl.ds(pl.multiple_of(t * 256, 256), 256)
+        for c in range(chips):
+            for part in range(2):
+                at[pl.ds(part * (d // 2) + c * LANES, LANES), r] = a[r, pl.ds((2 * c + part) * LANES, LANES)].T
+        return 0
+    lax.fori_loop(0, tokens // 256, turn, 0)
+    a_copy = pltpu.make_async_copy(at, a_out.at[0], misc.at[1])
     a_copy.start()
 
     def w_loads(l, j, slot):
@@ -154,7 +166,7 @@
                 stage[half, 1] = jnp.dot(rows_a, wchunk[slot, 1], preferred_element_type=F32)
                 if with_hidden:
                     gate, up = stage[half, 0], stage[half, 1]
-                    hidden[r, pl.ds(j * width, width)] = (jax.nn.silu(gate) * up).astype(BF16)
+                    hidden[r, pl.ds(j * width, width)] = (gate * sigmoid(gate) * up).astype(BF16)
                 for one in outs(t):
                     one.start()
                 return 0
@@ -201,10 +213,11 @@
     lax.fori_loop(0, tiles, down_step, 0)
     h_copy = pltpu.make_async_copy(h, h_out, misc.at[2])
     h_copy.start()
-    a_copy = pltpu.make_async_copy(a, a_out.at[1], misc.at[1])
-    a_copy.start()
     pass_on(4)
     begin(5)
+    lax.fori_loop(0, tokens // 256, turn, 0)
+    a_copy = pltpu.make_async_copy(at, a_out.at[1], misc.at[1])
+    a_copy.start()
     hand_over(3)
     hand_over(4)
     complete(3)
@@ -237,14 +250,14 @@
         name="forward",
         out_shape=(
             sds((layers, d, ff), BF16), sds((layers, d, ff), BF16), sds((layers, ff, d), BF16),
-            sds((layers, tokens, d), BF16), sds((tokens, d), BF16),
+            sds((layers, d, tokens), BF16), sds((tokens, d), BF16),
             sds((layers, chunks, tokens, width), F32), sds((layers, chunks, tokens, width), F32),
         ),
         in_specs=[ANY] * 4,
         out_specs=(ANY,) * 7,
         scratch_shapes=[
             pltpu.VMEM(wg.shape, BF16), pltpu.VMEM(wu.shape, BF16), pltpu.VMEM(wd.shape, BF16),
-            pltpu.VMEM((tokens, d), BF16), pltpu.VMEM((tokens, d), BF16), pltpu.VMEM((tokens, ff), BF16),
+            pltpu.VMEM((tokens, d), BF16), pltpu.VMEM((tokens, d), BF16), pltpu.VMEM((d, tokens), BF16), pltpu.VMEM((tokens, ff), BF16),
             pltpu.VMEM((2, 2, d, width), BF16), pltpu.VMEM((ff, d), BF16), pltpu.VMEM((2, 2, tile, width), F32),
             dma((3 * layers, 9)), dma((3 * layers, 9)), dma((3 * layers,)), dma((3 * layers,)),
             dma((2, 2, chips)), dma((2, 2)), dma((3 + chunks * chips,)),
@@ -253,13 +266,16 @@
     )(x, wg, wu, wd)
 
 
-SLOTS = 4
+SLOTS = 6
+PAIR_SLOTS = 4
+AHEAD = 4
+PAIR_LAG, PASS_LAG, FINAL_LAG = 1, 3, 5
 
 
 def backward_kernel(n, dy_ref, g_ref, u_ref, d_ref, a_ref, h_ref, gate_ref, up_ref, gg_out, gu_out, gd_out, sq_out,
-                    ct, at, nat, da, hid, hid_t, dg, du, dh, stage, wd, wgu, own, out_p, in_p, out_1, in_1, out_2, in_2, fin,
+                    ct, at, hs, da, hid, hid_t, dg, du, dh, stage, wd, wgu, own, out_p, in_p, out_1, in_1, out_2, in_2, fin,
                     gg, gu, gd, sq, squares,
-                    stage_sem, wd_sem, wgu_sem, p_send, p_recv, s1_send, s1_recv, s2_send, s2_recv, f_send, f_recv, q_send, q_recv, misc):
+                    stage_sem, wd_sem, wgu_sem, h_sem, p_send, p_recv, s1_send, s1_recv, s2_send, s2_recv, f_send, f_recv, q_send, q_recv, misc):
     me, chip, core, partner, right, left, far = places(n)
     layers, chunks, tokens, width = gate_ref.shape
     d = dy_ref.shape[1]
@@ -277,7 +293,7 @@
 
     def stage_loads(s):
         jj, t = s // tiles, lax.rem(s, tiles)
-        slot = lax.rem(s, 2)
+        slot = lax.rem(s, AHEAD)
         r = pl.ds(pl.multiple_of(t * tile, tile), tile)
         return [pltpu.make_async_copy(ref.at[layer_of(jj), lax.rem(jj, chunks), r], stage.at[slot, i], stage_sem.at[slot, i])
                 for i, ref in enumerate((gate_ref, up_ref))]
@@ -293,42 +309,40 @@
                                       wgu.at[slot, i, :, pl.ds(c * LANES, LANES)], wgu_sem.at[slot, i, c])
                 for i, ref in enumerate((g_ref, u_ref)) for c in range(chips)]
 
-    first = [pltpu.make_async_copy(a_ref.at[layers - 1], nat, misc.at[0]), pltpu.make_async_copy(dy_ref, ct, misc.at[1])]
-    for one in first + stage_loads(0) + wd_loads(0) + wgu_loads(0):
+    def at_load(l):
+        return pltpu.make_async_copy(a_ref.at[l], at, misc.at[0])
+
+    def h_load(t):
+        slot = lax.rem(t, AHEAD)
+        return pltpu.make_async_copy(h_ref.at[pl.ds(pl.multiple_of(t * sub, sub), sub)], hs.at[slot], h_sem.at[slot])
+
+    first = [pltpu.make_async_copy(dy_ref, ct, misc.at[1])]
+    for one in first + wd_loads(0) + wgu_loads(0) + [one for s in range(AHEAD) for one in stage_loads(s)]:
         one.start()
+    at_load(layers - 1).start()
+    for t in range(AHEAD):
+        h_load(t).start()
 
     barrier = pltpu.get_barrier_semaphore()
     others = [lax.rem(me + k, n) for k in range(1, n)]
     for other in others:
         pl.semaphore_signal(barrier, inc=1, device_id={"dp": other}, device_id_type=MESH)
-    pl.semaphore_wait(barrier, n - 1)
 
     def zero(t, _):
         da[pl.ds(pl.multiple_of(t * 128, 128), 128), :] = jnp.zeros((128, d), F32)
         return 0
     lax.fori_loop(0, tokens // 128, zero, 0)
     sq[...] = jnp.zeros_like(sq)
-
-    def turn(t, _):
-        r = pl.ds(pl.multiple_of(t * sub, sub), sub)
-        for c in range(chips):
-            for hh in range(2):
-                piece = nat[r, pl.ds((2 * c + hh) * LANES, LANES)]
-                at[pl.ds(hh * half + c * LANES, LANES), r] = piece.T
-        return 0
-
+    pl.semaphore_wait(barrier, n - 1)
     for one in first:
         one.wait()
-    lax.fori_loop(0, tokens // sub, turn, 0)
-    load_h = pltpu.make_async_copy(h_ref, nat, misc.at[0])
-    load_h.start()
 
     def remote(src, dst, ss, rs, to):
         return pltpu.make_async_remote_copy(src, dst, ss, rs, device_id={"dp": to}, device_id_type=MESH)
 
     def p_copy(k):
-        s = lax.rem(k, SLOTS)
-        return remote(out_p.at[s], in_p.at[s], p_send.at[s], p_recv.at[s], partner)
+        o, s = lax.rem(k, 2), lax.rem(k, PAIR_SLOTS)
+        return remote(out_p.at[o], in_p.at[s], p_send.at[o], p_recv.at[s], partner)
 
     def s1_copy(k, way):
         s = lax.rem(k, SLOTS)
@@ -342,7 +356,7 @@
     block_r, block_l, block_f = (lax.rem(chip + k, chips) for k in (1, chips - 1, 2))
 
     def pair_step(k):
-        s = lax.rem(k, SLOTS)
+        s, p = lax.rem(k, SLOTS), lax.rem(k, PAIR_SLOTS)
         p_copy(k).wait_recv()
 
         @pl.when(k >= SLOTS)
@@ -351,11 +365,11 @@
             s1_copy(k - SLOTS, 1).wait_send()
         for way in range(2):
             rows = pl.ds(way * mid, mid)
-            out_1[s, way] = (own[s, block_f, rows, :] + in_p[s, block_f, rows, :].astype(F32)).astype(BF16)
+            out_1[s, way] = (own[s, block_f, rows, :] + in_p[p, block_f, rows, :].astype(F32)).astype(BF16)
         s1_copy(k, 0).start()
         s1_copy(k, 1).start()
         for block in (block_r, block_l, chip):
-            own[s, block] += in_p[s, block].astype(F32)
+            own[s, block] += in_p[p, block].astype(F32)
 
     def pass_step(k):
         s = lax.rem(k, SLOTS)
@@ -429,45 +443,45 @@
         rows = pl.ds(pl.multiple_of(which * half, half), half)
         return jnp.dot(at[rows, :], (dg if kind == 1 else du)[...], preferred_element_type=F32)
 
-    def tick(k, kind, maybe):
-        s = lax.rem(k, SLOTS)
-
-        @pl.when(k >= SLOTS)
-        def _():
-            p_copy(k - SLOTS).wait_send()
-        store(kind, out_p, s, product(kind, 1 - core))
-        p_copy(k).start()
-        store(kind, own, s, product(kind, core))
-
+    def tick(k, kind):
         def run(step, lag, *more):
-            if maybe and lag > kind:
+            if lag > kind:
                 pl.when(k >= lag)(lambda: step(k - lag, *more))
             else:
                 step(k - lag, *more)
-        run(pair_step, 1)
-        run(pass_step, 2)
-        run(final_step, 3, kind)
+
+        @pl.when(k >= 2)
+        def _():
+            p_copy(k - 2).wait_send()
+        store(kind, out_p, lax.rem(k, 2), product(kind, 1 - core))
+        p_copy(k).start()
+        run(pair_step, PAIR_LAG)
+        run(pass_step, PASS_LAG)
+        store(kind, own, lax.rem(k, SLOTS), product(kind, core))
+        run(final_step, FINAL_LAG, (kind - FINAL_LAG) % 3)
 
     def chunk(jj, _):
         l, slot = layer_of(jj), lax.rem(jj, 2)
 
         @pl.when(jj == chunks)
         def _():
-            load_h.wait()
+            at_load(0).start()
 
             def to_h(t, _):
-                r = pl.ds(pl.multiple_of(t * 128, 128), 128)
-                wide = nat[r, :].astype(F32)
-                grad = da[r, :]
-                scale = lax.rsqrt(jnp.mean(wide * wide, -1, keepdims=True) + 1e-6)
-                back = grad * scale - wide * (scale * scale * scale * jnp.mean(grad * wide, -1, keepdims=True))
-                ct[r, :] = (ct[r, :].astype(F32) + back.astype(BF16).astype(F32)).astype(BF16)
+                h_load(t).wait()
+                for e in range(sub // 64):
+                    here = pl.ds(pl.multiple_of(t * sub + e * 64, 64), 64)
+                    wide = hs[lax.rem(t, AHEAD), pl.ds(e * 64, 64), :].astype(F32)
+                    grad = da[here, :]
+                    scale = lax.rsqrt(jnp.mean(wide * wide, -1, keepdims=True) + 1e-6)
+                    back = grad * scale - wide * (scale * scale * scale * jnp.mean(grad * wide, -1, keepdims=True))
+                    ct[here, :] = (ct[here, :].astype(F32) + back).astype(BF16)
+
+                @pl.when(t + AHEAD < tokens // sub)
+                def _():
+                    h_load(t + AHEAD).start()
                 return 0
-            lax.fori_loop(0, tokens // 128, to_h, 0)
-            load_a = pltpu.make_async_copy(a_ref.at[0], nat, misc.at[0])
-            load_a.start()
-            load_a.wait()
-            lax.fori_loop(0, tokens // sub, turn, 0)
+            lax.fori_loop(0, tokens // sub, to_h, 0)
 
         for one in wd_loads(jj):
             one.wait()
@@ -489,14 +503,9 @@
 
         def step(t, _):
             s = jj * tiles + t
-            st = lax.rem(s, 2)
+            st = lax.rem(s, AHEAD)
             for one in stage_loads(s):
                 one.wait()
-
-            @pl.when(s + 1 < total * tiles)
-            def _():
-                for one in stage_loads(s + 1):
-                    one.start()
             for q in range(tile // sub):
                 r = pl.ds(pl.multiple_of(t * tile + q * sub, sub), sub)
                 dh[q] = lax.dot_general(ct[r, :], wd[slot], NT, preferred_element_type=F32)
@@ -505,37 +514,51 @@
                     there = pl.ds(pl.multiple_of(t * tile + q * sub + e * 32, 32), 32)
                     gate, up = stage[st, 0, here, :], stage[st, 1, here, :]
                     back = dh[q, pl.ds(e * 32, 32), :].astype(BF16).astype(F32)
-                    sig = jax.nn.sigmoid(gate)
+                    sig = sigmoid(gate)
                     silu = gate * sig
-                    hid[there, :] = (silu * up).astype(BF16)
+                    hid[q, pl.ds(e * 32, 32), :] = (silu * up).astype(BF16)
                     du[there, :] = (back * silu).astype(BF16)
                     dg[there, :] = (back * up * (sig + silu * (1.0 - sig))).astype(BF16)
-                turned = hid[r, :].T
+                turned = hid[q].T
                 for c in range(chips):
                     for hh in range(2):
                         hid_t[pl.ds(hh * (width // 2) + c * mid, mid), r] = turned[c * LANES + hh * mid:c * LANES + (hh + 1) * mid, :]
+
+            @pl.when(s + AHEAD < total * tiles)
+            def _():
+                for one in stage_loads(s + AHEAD):
+                    one.start()
             return 0
         lax.fori_loop(0, tiles, step, 0)
 
-        @pl.when(jj < chunks)
-        def _():
+        @pl.when(lax.rem(jj, chunks) == 0)
+        def _():
+            at_load(layer_of(jj)).wait()
+
+        def back(part):
             def back_step(t, _):
                 r = pl.ds(pl.multiple_of(t * tile, tile), tile)
                 da[r, :] += (lax.dot_general(dg[r, :], wgu[slot, 0], NT, preferred_element_type=F32)
                              + lax.dot_general(du[r, :], wgu[slot, 1], NT, preferred_element_type=F32))
                 return 0
-            lax.fori_loop(0, tiles, back_step, 0)
-
-        for kind in range(3):
-            tick(jj * 3 + kind, kind, True)
+
+            @pl.when(jj < chunks)
+            def _():
+                lax.fori_loop(part * tiles // 2, (part + 1) * tiles // 2, back_step, 0)
+
+        tick(jj * 3, 0)
+        back(0)
+        tick(jj * 3 + 1, 1)
+        back(1)
+        tick(jj * 3 + 2, 2)
         return 0
     lax.fori_loop(0, total, chunk, 0)
 
     last = 3 * total
     pair_step(last - 1)
-    pass_step(last - 2)
-    final_step(last - 3, 0)
-    pass_step(last - 1)
+    for k in range(last - PASS_LAG, last):
+        pass_step(k)
+        final_step(k - 2, (k - 2) % 3)
     final_step(last - 2, 1)
     final_step(last - 1, 2)
 
@@ -572,8 +595,9 @@
     squares[n] = jnp.broadcast_to(jnp.sum(whole), (8, LANES))
     outs.append(pltpu.make_async_copy(squares.at[n], sq_out, misc.at[5]))
     outs[-1].start()
+    for k in range(last - 2, last):
+        p_copy(k).wait_send()
     for k in range(last - SLOTS, last):
-        p_copy(k).wait_send()
         for way in range(2):
             s1_copy(k, way).wait_send()
             s2_copy(k, way).wait_send()
@@ -601,15 +625,15 @@
         in_specs=[ANY] * 8,
         out_specs=(ANY,) * 4,
         scratch_shapes=[
-            v((tokens, d), BF16), v((d, tokens), BF16), v((tokens, d), BF16), v((tokens, d), F32),
-            v((tokens, width), BF16), v((width, tokens), BF16), v((tokens, width), BF16), v((tokens, width), BF16),
-            v((tile // 256, 256, width), F32), v((2, 2, tile, width), F32), v((2, width, d), BF16), v((2, 2, d, width), BF16),
-            v((SLOTS, chips, LANES, width), F32), v((SLOTS, chips, LANES, width), BF16), v((SLOTS, chips, LANES, width), BF16),
+            v((tokens, d), BF16), v((d, tokens), BF16), v((AHEAD, 256, d), BF16), v((tokens, d), F32),
+            v((tile // 256, 256, width), BF16), v((width, tokens), BF16), v((tokens, width), BF16), v((tokens, width), BF16),
+            v((tile // 256, 256, width), F32), v((AHEAD, 2, tile, width), F32), v((2, width, d), BF16), v((2, 2, d, width), BF16),
+            v((SLOTS, chips, LANES, width), F32), v((2, chips, LANES, width), BF16), v((PAIR_SLOTS, chips, LANES, width), BF16),
             v((SLOTS, 2, mid, width), BF16), v((SLOTS, 2, mid, width), BF16),
             v((SLOTS, 2, LANES, width), BF16), v((SLOTS, 2, LANES, width), BF16),
             v((layers, chunks, LANES, width), BF16),
             *(v(*g_) for g_ in grads), v((8, width), F32), v((n + 1, 8, LANES), F32),
-            dma((2, 2)), dma((2, chips)), dma((2, 2, chips)), dma((SLOTS,)), dma((SLOTS,)),
+            dma((AHEAD, 2)), dma((2, chips)), dma((2, 2, chips)), dma((AHEAD,)), dma((2,)), dma((PAIR_SLOTS,)),
             dma((SLOTS, 2)), dma((SLOTS, 2)), dma((SLOTS, 2)), dma((SLOTS, 2)),
             dma((layers, chunks, 2)), dma((layers, chunks, 2)), dma((n - 1,)), dma((n - 1,)), dma((6,)),
         ],

time: 423 us -> 353 us (0.83)
  Pallas kernels: 404 us -> 335 us
    pallas_call x1, Pallas kernels: 257 us -> 189 us  [backward(): pl.pallas_call(functools.partial(backward_kernel, n), name='backward', ou...]
where the time goes in v2:
time: 353 us
  Pallas kernels  335 us (95%)
  other arithmetic  13 us (4%)
    pallas_call x1, Pallas kernels, backward(): pl.pallas_call(functools.partial(backward_kernel, n), name='backward', ou...  189 us
    pallas_call x1, Pallas kernels, forward(): pl.pallas_call(functools.partial(forward_kernel, n), name='forward', out_...  147 us
    convert_element_type x2, other arithmetic, adamw(): return ((w - 0.02 * step).astype(BF16), m, v)  13 us

profile of v2, /device:TPU:113, one launch (start us, length us, event | category | flops | bytes accessed | tf_op | source)
XLA Modules:
  0.0 353.2 jit_solution(9365318483217324715)
XLA Ops:
  0.6 146.8 %forward.1 = (bf16[2,1024,2560]{2,1,0:T(8,128)(2,1)}, bf16[2,1024,2560]{2,1,0:T(8,128)(2,1)}, bf16[2,2560,1024]{2,1,0:T(8,128)(2,1)}, bf16[2,1024,2048]{2,1,0:T(...) custom-call(bf16[2048,1024]{1,0:T(8,128)(2,1)} %bitcast.4, ...), custom_call_target="tpu_custom_call" | custom-call | tf_op jit(solution)/shard_map/forward/pallas_call | solution.py:248
  147.5 0.0 copy-start
  147.5 0.0 copy-start.3
  147.5 188.5 %backward.1 = (bf16[2,128,2560]{2,1,0:T(8,128)(2,1)}, bf16[2,128,2560]{2,1,0:T(8,128)(2,1)}, bf16[2,320,1024]{2,1,0:T(8,128)(2,1)}, f32[8,128]{1,0:T(8,128)}) custom-call(bf16[2048,1024]{1,0:T(8,128)(2,1)} %bitcast.3, bf16[2,1024,2560]{2,1,0:T(8,128)(2,1)} %get-tuple-element.20.g_ref, bf16[2,1024,2560]{2,1,0:T(8,128)(2,1)} %get-tuple-element.21.u_ref, ...), custom_call_target="tpu_custom_call" | custom-call | tf_op jit(solution)/shard_map/backward/pallas_call | solution.py:621
  336.0 1.2 slice.3
  337.9 0.0 copy-done
  337.9 0.0 copy-done.3
  337.9 0.0 copy-start.1
  338.0 0.0 copy-start.2
  338.0 0.0 copy-start.4
  338.0 0.0 copy-start.5
  338.0 0.0 copy-start.6
  338.0 0.0 copy-start.7
  338.0 0.0 copy-start.8
  338.0 6.4 %fusion.8 = (bf16[2,320,1024]{2,1,0:T(8,128)(2,1)}, f32[2,320,1024]{2,1,0:T(8,128)}, f32[2,320,1024]{2,1,0:T(8,128)}) fusion(bf16[2,320,1024]{2,1,0:T(8,128)(2,1)S(1)} %copy-done, f32[]{:T(128)} %bitcast.2, bf16[2,320,1024]{2,1,0:T(8,128)(2,1)} %get-tuple-element.30, f32[2,320,1024]{2,1,0:T(8,128)S(1)} %copy-done.3, f32[2,320,1024]{2,1,0:T(8,128)} %param.18), kind=kLoop, calls=%fused_computation.17 | loop fusion | flops 11141120 | bytes 14417924 | tf_op jit(solution)/shard_map/convert_element_type | solution.py:648
  344.4 0.0 copy-done.1
  344.4 0.0 copy-done.2
  344.4 0.0 copy-done.4
  344.4 0.0 copy-done.5
  344.4 1.1 copy-done.6
  345.5 0.7 copy-done.7
  346.3 0.3 copy-done.8
  346.6 6.6 %fusion.2 = (bf16[2,128,2560]{2,1,0:T(8,128)(2,1)}, f32[2,128,2560]{2,1,0:T(8,128)}, f32[2,128,2560]{2,1,0:T(8,128)}, bf16[2,128,2560]{2,1,0:T(8,128)(2,1)}, f32...) fusion(bf16[2,128,2560]{2,1,0:T(8,128)(2,1)S(1)} %copy-done.1, f32[]{:T(128)} %bitcast.2, ...), kind=kLoop, calls=%fused_computation.11 | loop fusion | flops 22282240 | bytes 28835844 | tf_op jit(solution)/shard_map/convert_element_type | solution.py:648
Async XLA Ops:
  147.5 190.5 %copy-start = (bf16[2,320,1024]{2,1,0:T(8,128)(2,1)S(1)}, bf16[2,320,1024]{2,1,0:T(8,128)(2,1)}, u32[]{:S(2)}) copy-start(bf16[2,320,1024]{2,1,0:T(8,128)(2,1)} %wd_ref.1) | copy-start | bytes 3932164
  147.5 190.5 %copy-start.3 = (f32[2,320,1024]{2,1,0:T(8,128)S(1)}, f32[2,320,1024]{2,1,0:T(8,128)}, u32[]{:S(2)}) copy-start(f32[2,320,1024]{2,1,0:T(8,128)} %param.21) | copy-start | bytes 7864324
  337.9 6.4 %copy-start.1 = (bf16[2,128,2560]{2,1,0:T(8,128)(2,1)S(1)}, bf16[2,128,2560]{2,1,0:T(8,128)(2,1)}, u32[]{:S(2)}) copy-start(bf16[2,128,2560]{2,1,0:T(8,128)(2,1)} %wg_ref.1) | copy-start | bytes 3932164
  338.0 6.4 %copy-start.2 = (bf16[2,128,2560]{2,1,0:T(8,128)(2,1)S(1)}, bf16[2,128,2560]{2,1,0:T(8,128)(2,1)}, u32[]{:S(2)}) copy-start(bf16[2,128,2560]{2,1,0:T(8,128)(2,1)} %wu_ref.1) | copy-start | bytes 3932164
  338.0 6.4 %copy-start.4 = (f32[2,128,2560]{2,1,0:T(8,128)S(1)}, f32[2,128,2560]{2,1,0:T(8,128)}, u32[]{:S(2)}) copy-start(f32[2,128,2560]{2,1,0:T(8,128)} %param.19) | copy-start | bytes 7864324
  338.0 6.4 %copy-start.5 = (f32[2,128,2560]{2,1,0:T(8,128)S(1)}, f32[2,128,2560]{2,1,0:T(8,128)}, u32[]{:S(2)}) copy-start(f32[2,128,2560]{2,1,0:T(8,128)} %param.16) | copy-start | bytes 7864324
  338.0 7.5 %copy-start.6 = (f32[2,128,2560]{2,1,0:T(8,128)S(1)}, f32[2,128,2560]{2,1,0:T(8,128)}, u32[]{:S(2)}) copy-start(f32[2,128,2560]{2,1,0:T(8,128)} %param.20) | copy-start | bytes 7864324
  338.0 8.3 %copy-start.7 = (f32[2,128,2560]{2,1,0:T(8,128)S(1)}, f32[2,128,2560]{2,1,0:T(8,128)}, u32[]{:S(2)}) copy-start(f32[2,128,2560]{2,1,0:T(8,128)} %param.17) | copy-start | bytes 7864324
  338.0 8.6 %copy-start.8 = (bf16[2,128,2560]{2,1,0:T(8,128)(2,1)S(1)}, bf16[2,128,2560]{2,1,0:T(8,128)(2,1)}, u32[]{:S(2)}) copy-start(bf16[2,128,2560]{2,1,0:T(8,128)(2,1)} %get-tuple-element.27) | copy-start | bytes 3932164

commit v3 on v2

--- a/solution.py
+++ b/solution.py
@@ -39,9 +39,9 @@
     return (wide * scale).astype(BF16)
 
 
-def forward_kernel(n, x_ref, wg_ref, wu_ref, wd_ref, g_ref, u_ref, d_ref, a_out, h_out, gate_out, up_out,
-                   own_g, own_u, own_d, h, a, at, hidden, wchunk, wdown, stage,
-                   send, recv, own_sem, out_sem, w_sem, stage_sem, misc):
+def forward_kernel(n, x_ref, wg_ref, wu_ref, wd_ref, g_ref, u_ref, d_ref, a_out, h_out, gate_out, up_out, hid_out,
+                   own_g, own_u, own_d, h, a, at, hidden, wchunk, wdown, stage, hid, hid_t,
+                   send, recv, own_sem, out_sem, w_sem, stage_sem, hid_sem, misc):
     me, chip, core, partner, right, left, far = places(n)
     layers = wg_ref.shape[0]
     tokens, d = x_ref.shape
@@ -161,17 +161,37 @@
                 def _():
                     for one in outs(t):
                         one.wait()
-                rows_a = a[r, :]
-                stage[half, 0] = jnp.dot(rows_a, wchunk[slot, 0], preferred_element_type=F32)
-                stage[half, 1] = jnp.dot(rows_a, wchunk[slot, 1], preferred_element_type=F32)
-                if with_hidden:
-                    gate, up = stage[half, 0], stage[half, 1]
-                    hidden[r, pl.ds(j * width, width)] = (gate * sigmoid(gate) * up).astype(BF16)
+                for q in range(tile // 256):
+                    rows_a = a[pl.ds(pl.multiple_of(t * tile + q * 256, 256), 256), :]
+                    for i in range(2):
+                        stage[half, i, pl.ds(q * 256, 256), :] = jnp.dot(rows_a, wchunk[slot, i], preferred_element_type=F32)
+                    for e in range(256 // 32):
+                        here = pl.ds(q * 256 + e * 32, 32)
+                        gate, up = stage[half, 0, here, :], stage[half, 1, here, :]
+                        sig = sigmoid(gate)
+                        silu = gate * sig
+                        value = (silu * up).astype(BF16)
+                        hid[q, pl.ds(e * 32, 32), :] = value
+                        if with_hidden:
+                            hidden[pl.ds(pl.multiple_of(t * tile + q * 256 + e * 32, 32), 32), pl.ds(j * width, width)] = value
+                        stage[half, 0, here, :] = silu
+                        stage[half, 1, here, :] = up * (sig + silu * (1.0 - sig))
+                    turned = hid[q].T
+                    to = pl.ds(pl.multiple_of(t * tile + q * 256, 256), 256)
+                    for c in range(chips):
+                        for hh in range(2):
+                            hid_t[slot, pl.ds(hh * (width // 2) + c * (LANES // 2), LANES // 2), to] = \
+                                turned[c * LANES + hh * (LANES // 2):c * LANES + (hh + 1) * (LANES // 2), :]
                 for one in outs(t):
                     one.start()
                 return 0
+            if j >= 2:
+                pltpu.make_async_copy(hid_t.at[slot], hid_out.at[l, j], hid_sem.at[slot]).wait()
             lax.fori_loop(0, tiles, step, 0)
+            pltpu.make_async_copy(hid_t.at[slot], hid_out.at[l, j], hid_sem.at[slot]).start()
             between(j)
+        for slot in range(2):
+            pltpu.make_async_copy(hid_t.at[slot], hid_out.at[l, 0], hid_sem.at[slot]).wait()
         for half in range(2):
             for i, o in enumerate((gate_out, up_out)):
                 pltpu.make_async_copy(stage.at[half, i], o.at[l, 0, pl.ds(0, tile)], stage_sem.at[half, i]).wait()
@@ -252,15 +272,17 @@
             sds((layers, d, ff), BF16), sds((layers, d, ff), BF16), sds((layers, ff, d), BF16),
             sds((layers, d, tokens), BF16), sds((tokens, d), BF16),
             sds((layers, chunks, tokens, width), F32), sds((layers, chunks, tokens, width), F32),
+            sds((layers, chunks, width, tokens), BF16),
         ),
         in_specs=[ANY] * 4,
-        out_specs=(ANY,) * 7,
+        out_specs=(ANY,) * 8,
         scratch_shapes=[
             pltpu.VMEM(wg.shape, BF16), pltpu.VMEM(wu.shape, BF16), pltpu.VMEM(wd.shape, BF16),
             pltpu.VMEM((tokens, d), BF16), pltpu.VMEM((tokens, d), BF16), pltpu.VMEM((d, tokens), BF16), pltpu.VMEM((tokens, ff), BF16),
             pltpu.VMEM((2, 2, d, width), BF16), pltpu.VMEM((ff, d), BF16), pltpu.VMEM((2, 2, tile, width), F32),
+            pltpu.VMEM((tile // 256, 256, width), BF16), pltpu.VMEM((2, width, tokens), BF16),
             dma((3 * layers, 9)), dma((3 * layers, 9)), dma((3 * layers,)), dma((3 * layers,)),
-            dma((2, 2, chips)), dma((2, 2)), dma((3 + chunks * chips,)),
+            dma((2, 2, chips)), dma((2, 2)), dma((2,)), dma((3 + chunks * chips,)),
         ],
         compiler_params=pltpu.CompilerParams(collective_id=0, has_side_effects=True, vmem_limit_bytes=60 * 1024 * 1024),
     )(x, wg, wu, wd)
@@ -272,8 +294,8 @@
 PAIR_LAG, PASS_LAG, FINAL_LAG = 1, 3, 5
 
 
-def backward_kernel(n, dy_ref, g_ref, u_ref, d_ref, a_ref, h_ref, gate_ref, up_ref, gg_out, gu_out, gd_out, sq_out,
-                    ct, at, hs, da, hid, hid_t, dg, du, dh, stage, wd, wgu, own, out_p, in_p, out_1, in_1, out_2, in_2, fin,
+def backward_kernel(n, dy_ref, g_ref, u_ref, d_ref, a_ref, h_ref, gate_ref, up_ref, hid_ref, gg_out, gu_out, gd_out, sq_out,
+                    ct, at, hs, da, hid_t, dg, du, dh, stage, wd, wgu, own, out_p, in_p, out_1, in_1, out_2, in_2, fin,
                     gg, gu, gd, sq, squares,
                     stage_sem, wd_sem, wgu_sem, h_sem, p_send, p_recv, s1_send, s1_recv, s2_send, s2_recv, f_send, f_recv, q_send, q_recv, misc):
     me, chip, core, partner, right, left, far = places(n)
@@ -316,12 +338,12 @@
         slot = lax.rem(t, AHEAD)
         return pltpu.make_async_copy(h_ref.at[pl.ds(pl.multiple_of(t * sub, sub), sub)], hs.at[slot], h_sem.at[slot])
 
+    def hid_load(jj):
+        return pltpu.make_async_copy(hid_ref.at[layer_of(jj), lax.rem(jj, chunks)], hid_t, misc.at[2])
+
     first = [pltpu.make_async_copy(dy_ref, ct, misc.at[1])]
-    for one in first + wd_loads(0) + wgu_loads(0) + [one for s in range(AHEAD) for one in stage_loads(s)]:
+    for one in first + wd_loads(0) + stage_loads(0) + stage_loads(1):
         one.start()
-    at_load(layers - 1).start()
-    for t in range(AHEAD):
-        h_load(t).start()
 
     barrier = pltpu.get_barrier_semaphore()
     others = [lax.rem(me + k, n) for k in range(1, n)]
@@ -336,6 +358,11 @@
     pl.semaphore_wait(barrier, n - 1)
     for one in first:
         one.wait()
+    for one in stage_loads(2) + stage_loads(3) + [hid_load(0)] + wgu_loads(0):
+        one.start()
+    at_load(layers - 1).start()
+    for t in range(AHEAD):
+        h_load(t).start()
 
     def remote(src, dst, ss, rs, to):
         return pltpu.make_async_remote_copy(src, dst, ss, rs, device_id={"dp": to}, device_id_type=MESH)
@@ -486,11 +513,6 @@
         for one in wd_loads(jj):
             one.wait()
 
-        @pl.when(jj < chunks)
-        def _():
-            for one in wgu_loads(jj):
-                one.wait()
-
         @pl.when(jj + 1 < total)
         def _():
             for one in wd_loads(jj + 1):
@@ -512,17 +534,9 @@
                 for e in range(sub // 32):
                     here = pl.ds(q * sub + e * 32, 32)
                     there = pl.ds(pl.multiple_of(t * tile + q * sub + e * 32, 32), 32)
-                    gate, up = stage[st, 0, here, :], stage[st, 1, here, :]
                     back = dh[q, pl.ds(e * 32, 32), :].astype(BF16).astype(F32)
-                    sig = sigmoid(gate)
-                    silu = gate * sig
-                    hid[q, pl.ds(e * 32, 32), :] = (silu * up).astype(BF16)
-                    du[there, :] = (back * silu).astype(BF16)
-                    dg[there, :] = (back * up * (sig + silu * (1.0 - sig))).astype(BF16)
-                turned = hid[q].T
-                for c in range(chips):
-                    for hh in range(2):
-                        hid_t[pl.ds(hh * (width // 2) + c * mid, mid), r] = turned[c * LANES + hh * mid:c * LANES + (hh + 1) * mid, :]
+                    du[there, :] = (back * stage[st, 0, here, :]).astype(BF16)
+                    dg[there, :] = (back * stage[st, 1, here, :]).astype(BF16)
 
             @pl.when(s + AHEAD < total * tiles)
             def _():
@@ -546,7 +560,17 @@
             def _():
                 lax.fori_loop(part * tiles // 2, (part + 1) * tiles // 2, back_step, 0)
 
+        hid_load(jj).wait()
         tick(jj * 3, 0)
+
+        @pl.when(jj + 1 < total)
+        def _():
+            hid_load(jj + 1).start()
+
+        @pl.when(jj < chunks)
+        def _():
+            for one in wgu_loads(jj):
+                one.wait()
         back(0)
         tick(jj * 3 + 1, 1)
         back(1)
@@ -566,7 +590,7 @@
     copies = [remote(squares.at[me], squares.at[me], q_send.at[k], q_recv.at[k], other) for k, other in enumerate(others)]
     for one in copies:
         one.start()
-    outs = [pltpu.make_async_copy(a, b, misc.at[2 + i]) for i, (a, b) in enumerate(((gg, gg_out), (gu, gu_out)))]
+    outs = [pltpu.make_async_copy(a, b, misc.at[3 + i]) for i, (a, b) in enumerate(((gg, gg_out), (gu, gu_out)))]
     for one in outs:
         one.start()
     for l in range(layers):
@@ -585,7 +609,7 @@
                 def _():
                     f_copy(l, j, 0).wait_recv()
                     f_copy(l, j, 1).wait_recv()
-    outs.append(pltpu.make_async_copy(gd, gd_out, misc.at[4]))
+    outs.append(pltpu.make_async_copy(gd, gd_out, misc.at[5]))
     outs[-1].start()
     for one in copies:
         one.wait_recv()
@@ -593,7 +617,7 @@
     for k in range(1, n):
         whole = whole + squares[k]
     squares[n] = jnp.broadcast_to(jnp.sum(whole), (8, LANES))
-    outs.append(pltpu.make_async_copy(squares.at[n], sq_out, misc.at[5]))
+    outs.append(pltpu.make_async_copy(squares.at[n], sq_out, misc.at[6]))
     outs[-1].start()
     for k in range(last - 2, last):
         p_copy(k).wait_send()
@@ -607,7 +631,7 @@
         one.wait()
 
 
-def backward(n, dy, g, u, dn, a, h, gate, up):
+def backward(n, dy, g, u, dn, a, h, gate, up, hid):
     tokens, d = dy.shape
     layers, chunks, _, width = gate.shape
     ff = g.shape[2]
@@ -622,11 +646,11 @@
         functools.partial(backward_kernel, n),
         name="backward",
         out_shape=tuple(sds(*g_) for g_ in grads) + (sds((8, LANES), F32),),
-        in_specs=[ANY] * 8,
+        in_specs=[ANY] * 9,
         out_specs=(ANY,) * 4,
         scratch_shapes=[
             v((tokens, d), BF16), v((d, tokens), BF16), v((AHEAD, 256, d), BF16), v((tokens, d), F32),
-            v((tile // 256, 256, width), BF16), v((width, tokens), BF16), v((tokens, width), BF16), v((tokens, width), BF16),
+            v((width, tokens), BF16), v((tokens, width), BF16), v((tokens, width), BF16),
             v((tile // 256, 256, width), F32), v((AHEAD, 2, tile, width), F32), v((2, width, d), BF16), v((2, 2, d, width), BF16),
             v((SLOTS, chips, LANES, width), F32), v((2, chips, LANES, width), BF16), v((PAIR_SLOTS, chips, LANES, width), BF16),
             v((SLOTS, 2, mid, width), BF16), v((SLOTS, 2, mid, width), BF16),
@@ -635,10 +659,10 @@
             *(v(*g_) for g_ in grads), v((8, width), F32), v((n + 1, 8, LANES), F32),
             dma((AHEAD, 2)), dma((2, chips)), dma((2, 2, chips)), dma((AHEAD,)), dma((2,)), dma((PAIR_SLOTS,)),
             dma((SLOTS, 2)), dma((SLOTS, 2)), dma((SLOTS, 2)), dma((SLOTS, 2)),
-            dma((layers, chunks, 2)), dma((layers, chunks, 2)), dma((n - 1,)), dma((n - 1,)), dma((6,)),
+            dma((layers, chunks, 2)), dma((layers, chunks, 2)), dma((n - 1,)), dma((n - 1,)), dma((7,)),
         ],
         compiler_params=pltpu.CompilerParams(collective_id=1, has_side_effects=True, vmem_limit_bytes=60 * 1024 * 1024),
-    )(dy, g, u, dn, a, h, gate, up)
+    )(dy, g, u, dn, a, h, gate, up, hid)
 
 
 def adamw(w, m, v, g):
@@ -653,8 +677,8 @@
 
     def step(x, dy, *arrays):
         weights, m, v = (arrays[i : i + 3] for i in (0, 3, 6))
-        g, u, dn, a, h, gate, up = forward(n, x[0], *weights)
-        *gradients, squares = backward(n, dy[0], g, u, dn, a, h, gate, up)
+        g, u, dn, *saved = forward(n, x[0], *weights)
+        *gradients, squares = backward(n, dy[0], g, u, dn, *saved)
         factor = jnp.minimum(1.0, 0.5 * lax.rsqrt(squares[0, 0] / (n * sum(w.size for w in weights)) + 1e-30))
         new = [adamw(w.astype(F32), m, v, g.astype(F32) * factor) for w, m, v, g in zip(weights, m, v, gradients, strict=True)]
         return tuple(one[which] for which in range(3) for one in new)

time: 353 us -> 348 us (0.986)
  Pallas kernels: 335 us -> 330 us
    pallas_call x1, Pallas kernels: 189 us -> 181 us  [backward(): pl.pallas_call(functools.partial(backward_kernel, n), name='backward', ou...]
where the time goes in v3:
time: 348 us
  Pallas kernels  330 us (95%)
  other arithmetic  13 us (4%)
    pallas_call x1, Pallas kernels, backward(): pl.pallas_call(functools.partial(backward_kernel, n), name='backward', ou...  181 us
    pallas_call x1, Pallas kernels, forward(): pl.pallas_call(functools.partial(forward_kernel, n), name='forward', out_...  150 us
    convert_element_type x2, other arithmetic, adamw(): return ((w - 0.02 * step).astype(BF16), m, v)  13 us

profile of v3, /device:TPU:113, one launch (start us, length us, event | category | flops | bytes accessed | tf_op | source)
XLA Modules:
  0.0 348.1 jit_solution(4944000885263544667)
XLA Ops:
  0.6 149.7 %forward.1 = (bf16[2,1024,2560]{2,1,0:T(8,128)(2,1)}, bf16[2,1024,2560]{2,1,0:T(8,128)(2,1)}, bf16[2,2560,1024]{2,1,0:T(8,128)(2,1)}, bf16[2,1024,2048]{2,1,0:T(...) custom-call(bf16[2048,1024]{1,0:T(8,128)(2,1)} %bitcast.4, ...), custom_call_target="tpu_custom_call" | custom-call | tf_op jit(solution)/shard_map/forward/pallas_call | solution.py:268
  150.4 0.0 copy-start
  150.4 0.0 copy-start.3
  150.4 180.6 %backward.1 = (bf16[2,128,2560]{2,1,0:T(8,128)(2,1)}, bf16[2,128,2560]{2,1,0:T(8,128)(2,1)}, bf16[2,320,1024]{2,1,0:T(8,128)(2,1)}, f32[8,128]{1,0:T(8,128)}) custom-call(bf16[2048,1024]{1,0:T(8,128)(2,1)} %bitcast.3, bf16[2,1024,2560]{2,1,0:T(8,128)(2,1)} %get-tuple-element.21.g_ref, bf16[2,1024,2560]{2,1,0:T(8,128)(2,1)} %get-tuple-element.22.u_ref, ...), custom_call_target="tpu_custom_call" | custom-call | tf_op jit(solution)/shard_map/backward/pallas_call | solution.py:645
  331.0 1.2 slice.3
  332.9 0.0 copy-done
  332.9 0.0 copy-done.3
  332.9 0.0 copy-start.1
  332.9 0.0 copy-start.2
  332.9 0.0 copy-start.4
  332.9 0.0 copy-start.5
  332.9 0.0 copy-start.6
  333.0 0.0 copy-start.7
  333.0 0.0 copy-start.8
  333.0 6.4 %fusion.8 = (bf16[2,320,1024]{2,1,0:T(8,128)(2,1)}, f32[2,320,1024]{2,1,0:T(8,128)}, f32[2,320,1024]{2,1,0:T(8,128)}) fusion(bf16[2,320,1024]{2,1,0:T(8,128)(2,1)S(1)} %copy-done, f32[]{:T(128)} %bitcast.2, bf16[2,320,1024]{2,1,0:T(8,128)(2,1)} %get-tuple-element.32, f32[2,320,1024]{2,1,0:T(8,128)S(1)} %copy-done.3, f32[2,320,1024]{2,1,0:T(8,128)} %param.18), kind=kLoop, calls=%fused_computation.17 | loop fusion | flops 11141120 | bytes 14417924 | tf_op jit(solution)/shard_map/convert_element_type | solution.py:672
  339.3 0.0 copy-done.1
  339.3 0.0 copy-done.2
  339.3 0.0 copy-done.4
  339.3 0.0 copy-done.5
  339.4 1.1 copy-done.6
  340.5 0.7 copy-done.7
  341.2 0.3 copy-done.8
  341.5 6.6 %fusion.2 = (bf16[2,128,2560]{2,1,0:T(8,128)(2,1)}, f32[2,128,2560]{2,1,0:T(8,128)}, f32[2,128,2560]{2,1,0:T(8,128)}, bf16[2,128,2560]{2,1,0:T(8,128)(2,1)}, f32...) fusion(bf16[2,128,2560]{2,1,0:T(8,128)(2,1)S(1)} %copy-done.1, f32[]{:T(128)} %bitcast.2, ...), kind=kLoop, calls=%fused_computation.11 | loop fusion | flops 22282240 | bytes 28835844 | tf_op jit(solution)/shard_map/convert_element_type | solution.py:672
Async XLA Ops:
  150.4 182.5 %copy-start = (bf16[2,320,1024]{2,1,0:T(8,128)(2,1)S(1)}, bf16[2,320,1024]{2,1,0:T(8,128)(2,1)}, u32[]{:S(2)}) copy-start(bf16[2,320,1024]{2,1,0:T(8,128)(2,1)} %wd_ref.1) | copy-start | bytes 3932164
  150.4 182.5 %copy-start.3 = (f32[2,320,1024]{2,1,0:T(8,128)S(1)}, f32[2,320,1024]{2,1,0:T(8,128)}, u32[]{:S(2)}) copy-start(f32[2,320,1024]{2,1,0:T(8,128)} %param.21) | copy-start | bytes 7864324
  332.9 6.4 %copy-start.1 = (bf16[2,128,2560]{2,1,0:T(8,128)(2,1)S(1)}, bf16[2,128,2560]{2,1,0:T(8,128)(2,1)}, u32[]{:S(2)}) copy-start(bf16[2,128,2560]{2,1,0:T(8,128)(2,1)} %wg_ref.1) | copy-start | bytes 3932164
  332.9 6.4 %copy-start.2 = (bf16[2,128,2560]{2,1,0:T(8,128)(2,1)S(1)}, bf16[2,128,2560]{2,1,0:T(8,128)(2,1)}, u32[]{:S(2)}) copy-start(bf16[2,128,2560]{2,1,0:T(8,128)(2,1)} %wu_ref.1) | copy-start | bytes 3932164
  332.9 6.4 %copy-start.4 = (f32[2,128,2560]{2,1,0:T(8,128)S(1)}, f32[2,128,2560]{2,1,0:T(8,128)}, u32[]{:S(2)}) copy-start(f32[2,128,2560]{2,1,0:T(8,128)} %param.19) | copy-start | bytes 7864324
  332.9 6.4 %copy-start.5 = (f32[2,128,2560]{2,1,0:T(8,128)S(1)}, f32[2,128,2560]{2,1,0:T(8,128)}, u32[]{:S(2)}) copy-start(f32[2,128,2560]{2,1,0:T(8,128)} %param.16) | copy-start | bytes 7864324
  332.9 7.5 %copy-start.6 = (f32[2,128,2560]{2,1,0:T(8,128)S(1)}, f32[2,128,2560]{2,1,0:T(8,128)}, u32[]{:S(2)}) copy-start(f32[2,128,2560]{2,1,0:T(8,128)} %param.20) | copy-start | bytes 7864324
  333.0 8.3 %copy-start.7 = (f32[2,128,2560]{2,1,0:T(8,128)S(1)}, f32[2,128,2560]{2,1,0:T(8,128)}, u32[]{:S(2)}) copy-start(f32[2,128,2560]{2,1,0:T(8,128)} %param.17) | copy-start | bytes 7864324
  333.0 8.6 %copy-start.8 = (bf16[2,128,2560]{2,1,0:T(8,128)(2,1)S(1)}, bf16[2,128,2560]{2,1,0:T(8,128)(2,1)}, u32[]{:S(2)}) copy-start(bf16[2,128,2560]{2,1,0:T(8,128)(2,1)} %get-tuple-element.29) | copy-start | bytes 3932164

commit v4 on v3

--- a/solution.py
+++ b/solution.py
@@ -672,6 +672,29 @@
     return (w - 0.02 * step).astype(BF16), m, v
 
 
+def update_kernel(count, squares_ref, *refs):
+    factor = jnp.minimum(1.0, 0.5 * lax.rsqrt(squares_ref[0:1, 0:1] / count + 1e-30))
+    for i in range(3):
+        w, m, v, g = (refs[3 * which + i] for which in range(4))
+        new = adamw(w[0].astype(F32), m[0], v[0], g[0].astype(F32) * factor)
+        for which in range(3):
+            refs[12 + 3 * which + i][0] = new[which]
+
+
+def update(count, squares, weights, m, v, gradients):
+    parts = 4
+    specs = [pl.BlockSpec((1, w.shape[1] // parts, w.shape[2]), lambda l, r: (l, r, 0)) for w in weights]
+    return pl.pallas_call(
+        functools.partial(update_kernel, count),
+        name="update",
+        grid=(weights[0].shape[0], parts),
+        out_shape=[jax.ShapeDtypeStruct(w.shape, dtype) for dtype in (BF16, F32, F32) for w in weights],
+        in_specs=[pl.BlockSpec(squares.shape, lambda l, r: (0, 0))] + specs * 4,
+        out_specs=specs * 3,
+        compiler_params=pltpu.CompilerParams(vmem_limit_bytes=40_000 * 1024),
+    )(squares, *weights, *m, *v, *gradients)
+
+
 def solution(mesh):
     n = mesh.shape["dp"]
 
@@ -679,9 +702,7 @@
         weights, m, v = (arrays[i : i + 3] for i in (0, 3, 6))
         g, u, dn, *saved = forward(n, x[0], *weights)
         *gradients, squares = backward(n, dy[0], g, u, dn, *saved)
-        factor = jnp.minimum(1.0, 0.5 * lax.rsqrt(squares[0, 0] / (n * sum(w.size for w in weights)) + 1e-30))
-        new = [adamw(w.astype(F32), m, v, g.astype(F32) * factor) for w, m, v, g in zip(weights, m, v, gradients, strict=True)]
-        return tuple(one[which] for which in range(3) for one in new)
+        return tuple(update(n * sum(w.size for w in weights), squares, weights, m, v, gradients))
 
     states, cut = P(("rep", "dp"), None, None), P(None, "dp", None)
     return jax.shard_map(

time: 348 us -> 353 us (1.014)
  Pallas kernels: 330 us -> 344 us
  other arithmetic: 13 us -> 0 us
  local copies, waits for them, and re-layouts: 3.42 us -> 8.12 us
    pallas_call x0 -> x1, Pallas kernels: none -> 13.5 us  [update(): pl.pallas_call(functools.partial(update_kernel, count), name='update', gr...]
    convert_element_type x2 -> x0, other arithmetic: 13 us -> none  [adamw(): return ((w - 0.02 * step).astype(BF16), m, v)]
    unnamed x18, local copies, waits for them, and re-layouts: 2.24 us -> 8.12 us
where the time goes in v4:
time: 353 us
  Pallas kernels  344 us (97%)
  local copies, waits for them, and re-layouts  8.12 us (2%)
    pallas_call x1, Pallas kernels, backward(): pl.pallas_call(functools.partial(backward_kernel, n), name='backward', ou...  181 us
    pallas_call x1, Pallas kernels, forward(): pl.pallas_call(functools.partial(forward_kernel, n), name='forward', out_...  150 us
    pallas_call x1, Pallas kernels, update(): pl.pallas_call(functools.partial(update_kernel, count), name='update', gr...  13.5 us
    unnamed x18, local copies, waits for them, and re-layouts  8.12 us

profile of v4, /device:TPU:113, one launch (start us, length us, event | category | flops | bytes accessed | tf_op | source)
XLA Modules:
  0.0 352.8 jit_solution(2931744778813768270)
XLA Ops:
  0.6 149.7 %forward.1 = (bf16[2,1024,2560]{2,1,0:T(8,128)(2,1)}, bf16[2,1024,2560]{2,1,0:T(8,128)(2,1)}, bf16[2,2560,1024]{2,1,0:T(8,128)(2,1)}, bf16[2,1024,2048]{2,1,0:T(...) custom-call(bf16[2048,1024]{1,0:T(8,128)(2,1)} %bitcast.3, ...), custom_call_target="tpu_custom_call" | custom-call | tf_op jit(solution)/shard_map/forward/pallas_call | solution.py:268
  150.4 0.0 copy-start
  150.4 0.0 copy-start.1
  150.4 0.0 copy-start.2
  150.4 180.6 %backward.1 = (bf16[2,128,2560]{2,1,0:T(8,128)(2,1)}, bf16[2,128,2560]{2,1,0:T(8,128)(2,1)}, bf16[2,320,1024]{2,1,0:T(8,128)(2,1)}, f32[8,128]{1,0:T(8,128)}) custom-call(bf16[2048,1024]{1,0:T(8,128)(2,1)} %bitcast.2, bf16[2,1024,2560]{2,1,0:T(8,128)(2,1)} %get-tuple-element.21.g_ref, bf16[2,1024,2560]{2,1,0:T(8,128)(2,1)} %get-tuple-element.22.u_ref, ...), custom_call_target="tpu_custom_call" | custom-call | tf_op jit(solution)/shard_map/backward/pallas_call | solution.py:645
  331.0 0.0 copy-done
  331.0 0.0 copy-done.1
  331.0 0.0 copy-done.2
  331.0 0.0 copy-start.3
  331.0 1.7 copy-done.3
  332.8 0.0 copy-start.4
  332.8 1.7 copy-done.4
  334.5 0.0 copy-start.5
  334.5 1.3 copy-done.5
  335.8 0.0 copy-start.6
  335.8 1.3 copy-done.6
  337.1 0.0 copy-start.7
  337.1 1.3 copy-done.7
  338.5 0.0 copy-start.8
  338.5 0.7 copy-done.8
  339.1 13.5 %update.1 = (bf16[2,128,2560]{2,1,0:T(8,128)(2,1)}, bf16[2,128,2560]{2,1,0:T(8,128)(2,1)}, bf16[2,320,1024]{2,1,0:T(8,128)(2,1)}, f32[2,128,2560]{2,1,0:T(8,128)...) custom-call(f32[8,128]{1,0:T(8,128)S(1)} %copy-done.8, ...), custom_call_target="tpu_custom_call" | custom-call | tf_op jit(solution)/shard_map/update/pallas_call | solution.py:687
Async XLA Ops:
  150.4 180.6 %copy-start = (bf16[2,128,2560]{2,1,0:T(8,128)(2,1)S(1)}, bf16[2,128,2560]{2,1,0:T(8,128)(2,1)}, u32[]{:S(2)}) copy-start(bf16[2,128,2560]{2,1,0:T(8,128)(2,1)} %refs_0_.1) | copy-start | bytes 3932164
  150.4 180.6 %copy-start.1 = (bf16[2,128,2560]{2,1,0:T(8,128)(2,1)S(1)}, bf16[2,128,2560]{2,1,0:T(8,128)(2,1)}, u32[]{:S(2)}) copy-start(bf16[2,128,2560]{2,1,0:T(8,128)(2,1)} %refs_1_.1) | copy-start | bytes 3932164
  150.4 180.6 %copy-start.2 = (bf16[2,320,1024]{2,1,0:T(8,128)(2,1)S(1)}, bf16[2,320,1024]{2,1,0:T(8,128)(2,1)}, u32[]{:S(2)}) copy-start(bf16[2,320,1024]{2,1,0:T(8,128)(2,1)} %refs_2_.1) | copy-start | bytes 3932164
  331.0 1.7 copy-start.3
  332.8 1.7 copy-start.4
  334.5 1.3 copy-start.5
  335.8 1.3 copy-start.6
  337.1 1.3 copy-start.7
  338.5 0.7 copy-start.8
